TPU v7x, 32 devices: a 4x4x1 block of a 4x4x8 slice. The times are simulated.
32 devices in a mesh: fields: 1 (over z), col: 4 (over y), row: 8 (over x, core).
Axes of the slice: x: 4, y: 4, z: 1, core: 2. Of those that a mesh axis runs over, the one named last changes fastest.
The devices are a block of a 4x4x8 slice.
Arguments:
- field_u: bfloat16 [1, 512, 512, 512], P('fields', None, 'row', 'col')
- fac_a: bfloat16 [512, 512], P('fields')
- fac_b: bfloat16 [512, 512], P('fields')
- fac_c: bfloat16 [512, 512], P('fields')
- diag_d: float32 [512, 512, 512], P(('fields', 'row'), 'col')
Outputs:
- output: float32 [1, 512, 512, 512], P('fields', None, 'row', 'col')
All inputs are finite; a program needn't handle non-finite values.
Results may differ from a plain program's by a relative error of at most 0.00303378.
Values are sent between devices in bfloat16 or wider.
A program may use at most 768 MiB of HBM per device.

v0:
```python
import jax
import jax.numpy as jnp
from jax import lax
from jax.sharding import PartitionSpec as P


def solution(mesh):
    spec_field = P("fields", None, "row", "col")
    spec_factor = P("fields", None)
    spec_diag = P(("fields", "row"), "col", None)

    def local_apply(field_u, fac_a, fac_b, fac_c, diag_d):
        stage_one = jnp.einsum("ix,bxyz->biyz", fac_a, field_u, preferred_element_type=jnp.float32).astype(jnp.bfloat16)
        y_pencil = lax.all_to_all(stage_one, "row", 1, 2, tiled=True)
        stage_two = jnp.einsum("jy,biyz->bijz", fac_b, y_pencil, preferred_element_type=jnp.float32).astype(jnp.bfloat16)
        z_pencil = lax.all_to_all(stage_two, "col", 2, 3, tiled=True)
        stage_three = (jnp.einsum("kz,bijz->bijk", fac_c, z_pencil, preferred_element_type=jnp.float32) * diag_d).astype(jnp.bfloat16)
        stage_four = jnp.einsum("kz,bijk->bijz", fac_c, stage_three, preferred_element_type=jnp.float32).astype(jnp.bfloat16)
        back_y = lax.all_to_all(stage_four, "col", 3, 2, tiled=True)
        stage_five = jnp.einsum("jy,bijz->biyz", fac_b, back_y, preferred_element_type=jnp.float32).astype(jnp.bfloat16)
        back_x = lax.all_to_all(stage_five, "row", 2, 1, tiled=True)
        return jnp.einsum("ix,biyz->bxyz", fac_a, back_x, preferred_element_type=jnp.float32)

    return jax.shard_map(local_apply, mesh=mesh, in_specs=(spec_field, spec_factor, spec_factor, spec_factor, spec_diag), out_specs=spec_field, check_vma=False)
```

profile of v0, /device:TPU:97, one launch (start us, length us, event | category | flops | bytes accessed | tf_op | source)
XLA Modules:
  0.0 656.4 jit_solution(12178256569891881552)
XLA Ops:
  0.0 0.0 copy-start
  0.0 25.3 %convert_bitcast_fusion.3 = bf16[1,512,64,128]{1,3,2,0:T(8,128)(2,1)} fusion(bf16[512,64,128]{2,1,0:T(8,128)(2,1)} %bitcast.62, bf16[512,512]{1,0:T(8,128)(2,1)} %param.6), kind=kOutput, calls=%fused_computation.9 | convolution fusion | flops 4299161600 | bytes 17301504 | tf_op jit(solution)/shard_map/ix,bxyz->biyz/dot_general | solution.py:13
  25.3 12.1 %copy.35 = bf16[1,512,64,128]{3,2,0,1:T(8,128)(2,1)} copy(bf16[1,512,64,128]{1,3,2,0:T(8,128)(2,1)} %convert_bitcast_fusion.3) | data formatting | bytes 16777216 | tf_op jit(solution)/shard_map/convert_element_type | solution.py:13
  37.3 101.1 %all_to_all.60 = bf16[1,512,64,128]{3,2,0,1:T(8,128)(2,1)} all-to-all(bf16[1,512,64,128]{3,2,0,1:T(8,128)(2,1)} %copy.35), channel_id=1, replica_groups=mesh['fields'=1,'col'=4,'row'=8] {'row'}, dimensions={1} | all-to-all | bytes 16777216 | tf_op jit(solution)/shard_map/all_to_all | solution.py:14
  138.5 9.8 %copy.36 = bf16[1,64,8,64,128]{4,3,2,1,0:T(8,128)(2,1)} copy(bf16[1,64,8,64,128]{4,3,1,2,0:T(8,128)(2,1)} %bitcast.55) | data formatting | bytes 16777216 | tf_op jit(solution)/shard_map/all_to_all | solution.py:14
  148.3 0.0 copy-done
  148.3 10.3 %convert_bitcast_fusion.2 = bf16[1,64,512,128]{2,3,1,0:T(8,128)(2,1)} fusion(bf16[64,512,128]{2,1,0:T(8,128)(2,1)} %bitcast.60, bf16[512,512]{1,0:T(8,128)(2,1)S(1)} %copy-done), kind=kOutput, calls=%fused_computation.8 | convolution fusion | flops 4299161600 | bytes 17301504 | tf_op jit(solution)/shard_map/jy,biyz->bijz/dot_general | solution.py:15
  158.5 11.9 %copy.38 = bf16[1,64,512,128]{3,1,0,2:T(8,128)(2,1)} copy(bf16[1,64,512,128]{2,3,1,0:T(8,128)(2,1)} %convert_bitcast_fusion.2) | data formatting | bytes 16777216 | tf_op jit(solution)/shard_map/convert_element_type | solution.py:15
  170.4 101.8 %all_to_all.61 = bf16[1,64,512,128]{3,1,0,2:T(8,128)(2,1)} all-to-all(bf16[1,64,512,128]{3,1,0,2:T(8,128)(2,1)} %copy.38), channel_id=1, replica_groups=mesh['fields'=1,'col'=4,'row'=8] {'col'}, dimensions={2} | all-to-all | bytes 16777216 | tf_op jit(solution)/shard_map/all_to_all | solution.py:16
  272.2 12.2 %copy.39 = bf16[1,64,512,128]{3,2,1,0:T(8,128)(2,1)} copy(bf16[1,64,512,128]{3,1,0,2:T(8,128)(2,1)} %all_to_all.61) | data formatting | bytes 16777216 | tf_op jit(solution)/shard_map/all_to_all | solution.py:16
  284.4 0.0 copy-start.2
  284.4 12.0 %copy.40 = bf16[1,64,128,4,128]{2,4,3,1,0:T(8,128)(2,1)} copy(bf16[1,64,128,4,128]{4,2,3,1,0:T(8,128)(2,1)} %bitcast.56) | data formatting | bytes 16777216 | tf_op jit(solution)/shard_map/all_to_all | solution.py:16
  296.4 0.0 copy-done.2
  296.4 15.9 %convert_bitcast_fusion.1 = bf16[1,64,128,512]{3,2,1,0:T(8,128)(2,1)} fusion(f32[64,128,512]{2,1,0:T(8,128)} %param.9, bf16[64,128,512]{1,2,0:T(8,128)(2,1)} %bitcast.61, bf16[512,512]{1,0:T(8,128)(2,1)S(1)} %copy-done.2), kind=kOutput, calls=%fused_computation.7 | convolution fusion | flops 8602517504 | bytes 34078720 | tf_op jit(solution)/shard_map/kz,bijk->bijz/dot_general | solution.py:18
  312.3 12.1 %copy.42 = bf16[1,64,128,512]{2,1,0,3:T(8,128)(2,1)} copy(bf16[1,64,128,512]{3,2,1,0:T(8,128)(2,1)} %convert_bitcast_fusion.1) | data formatting | bytes 16777216 | tf_op jit(solution)/shard_map/convert_element_type | solution.py:18
  324.3 96.7 %all_to_all.62 = bf16[1,64,128,512]{2,1,0,3:T(8,128)(2,1)S(1)} all-to-all(bf16[1,64,128,512]{2,1,0,3:T(8,128)(2,1)} %copy.42), channel_id=1, replica_groups=mesh['fields'=1,'col'=4,'row'=8] {'col'}, dimensions={3} | all-to-all | bytes 16777216 | tf_op jit(solution)/shard_map/all_to_all | solution.py:19
  421.0 18.4 %copy.58 = bf16[1,64,128,4,128]{2,3,4,1,0:T(4,128)(2,1)} copy(bf16[1,64,128,4,128]{2,1,4,3,0:T(8,128)(2,1)S(1)} %bitcast.57) | data formatting | bytes 16777216 | tf_op jit(solution)/shard_map/all_to_all | solution.py:19
  439.4 13.1 %reshape.36 = bf16[64,512,128]{1,2,0:T(8,128)(2,1)} reshape(bf16[1,64,4,128,128]{3,2,4,1,0:T(4,128)(2,1)} %bitcast.58) | data formatting | bytes 16777216 | tf_op jit(solution)/shard_map/reshape.8
  452.5 10.1 %convert_bitcast_fusion = bf16[1,64,512,128]{2,3,1,0:T(8,128)(2,1)} fusion(bf16[64,512,128]{1,2,0:T(8,128)(2,1)} %reshape.36, bf16[512,512]{1,0:T(8,128)(2,1)S(1)} %copy-done), kind=kOutput, calls=%fused_computation.6 | convolution fusion | flops 4299161600 | bytes 17301504 | tf_op jit(solution)/shard_map/jy,bijz->biyz/dot_general | solution.py:20
  462.6 12.1 %copy.44 = bf16[1,64,512,128]{3,1,0,2:T(8,128)(2,1)} copy(bf16[1,64,512,128]{2,3,1,0:T(8,128)(2,1)} %convert_bitcast_fusion) | data formatting | bytes 16777216 | tf_op jit(solution)/shard_map/convert_element_type | solution.py:20
  474.7 101.3 %all_to_all.63 = bf16[1,64,512,128]{3,1,0,2:T(8,128)(2,1)} all-to-all(bf16[1,64,512,128]{3,1,0,2:T(8,128)(2,1)} %copy.44), channel_id=1, replica_groups=mesh['fields'=1,'col'=4,'row'=8] {'row'}, dimensions={2} | all-to-all | bytes 16777216 | tf_op jit(solution)/shard_map/all_to_all | solution.py:21
  576.0 12.2 %copy.45 = bf16[1,64,512,128]{3,2,1,0:T(8,128)(2,1)} copy(bf16[1,64,512,128]{3,1,0,2:T(8,128)(2,1)} %all_to_all.63) | data formatting | bytes 16777216 | tf_op jit(solution)/shard_map/all_to_all | solution.py:21
  588.1 0.0 copy-start.1
  588.1 9.6 %copy.46 = bf16[1,8,64,64,128]{4,3,2,1,0:T(8,128)(2,1)} copy(bf16[1,8,64,64,128]{4,3,1,2,0:T(8,128)(2,1)} %bitcast.59) | data formatting | bytes 16777216 | tf_op jit(solution)/shard_map/all_to_all | solution.py:21
  597.7 0.0 copy-done.1
  597.7 41.8 %convolution_bitcast_fusion = f32[1,512,64,128]{1,3,2,0:T(8,128)} fusion(bf16[512,64,128]{2,1,0:T(8,128)(2,1)} %bitcast.54, bf16[512,512]{1,0:T(8,128)(2,1)S(1)} %copy-done.1), kind=kOutput, calls=%fused_computation.1 | convolution fusion | flops 4294967296 | bytes 25690112 | tf_op jit(solution)/shard_map/ix,biyz->bxyz/dot_general | solution.py:22
  639.5 16.5 %copy.48 = f32[1,512,64,128]{3,2,1,0:T(8,128)} copy(f32[1,512,64,128]{1,3,2,0:T(8,128)} %convolution_bitcast_fusion) | data formatting | bytes 33554432 | tf_op jit(solution)/shard_map/ix,biyz->bxyz/transpose | solution.py:22
Async XLA Ops:
  0.0 148.3 %copy-start = (bf16[512,512]{1,0:T(8,128)(2,1)S(1)}, bf16[512,512]{1,0:T(8,128)(2,1)}, u32[]{:S(2)}) copy-start(bf16[512,512]{1,0:T(8,128)(2,1)} %param.7) | copy-start | bytes 1572868
  284.4 12.0 %copy-start.2 = (bf16[512,512]{1,0:T(8,128)(2,1)S(1)}, bf16[512,512]{1,0:T(8,128)(2,1)}, u32[]{:S(2)}) copy-start(bf16[512,512]{1,0:T(8,128)(2,1)} %param.8) | copy-start | bytes 1572868
  588.1 9.6 %copy-start.1 = (bf16[512,512]{1,0:T(8,128)(2,1)S(1)}, bf16[512,512]{1,0:T(8,128)(2,1)}, u32[]{:S(2)}) copy-start(bf16[512,512]{1,0:T(8,128)(2,1)} %param.6) | copy-start | bytes 1572868
where the time goes:
time: 668 us; the launch traced here: 656 us
  blocking collectives  401 us (60%)
  local copies, waits for them, and re-layouts  152 us (23%)
  matrix products  103 us (15%)
    all_to_all x1, blocking collectives, local_apply(): z_pencil = lax.all_to_all(stage_two, 'col', 2, 3, tiled=True)  102 us
    all_to_all x1, blocking collectives, local_apply(): back_x = lax.all_to_all(stage_five, 'row', 2, 1, tiled=True)  101 us
    all_to_all x1, blocking collectives, local_apply(): y_pencil = lax.all_to_all(stage_one, 'row', 1, 2, tiled=True)  101 us
    all_to_all x1, blocking collectives, local_apply(): back_y = lax.all_to_all(stage_four, 'col', 3, 2, tiled=True)  96.7 us
    dot_general x1, matrix products, local_apply(): jnp.einsum('ix,biyz->bxyz', fac_a, back_x, preferred_element_type=jnp.flo...  41.8 us
    dot_general x1, matrix products, local_apply(): jnp.einsum('ix,bxyz->biyz', fac_a, field_u, preferred_element_type=jnp.fl...  25.3 us
    all_to_all x2, local copies, waits for them, and re-layouts, local_apply(): z_pencil = lax.all_to_all(stage_two, 'col', 2, 3, tiled=True)  24.2 us
    all_to_all x2, local copies, waits for them, and re-layouts, local_apply(): back_x = lax.all_to_all(stage_five, 'row', 2, 1, tiled=True)  21.7 us

commit v1 on v0

v1 whole, which is shorter than its diff:
```python
import functools

import jax
import jax.numpy as jnp
from jax import lax
from jax.experimental import pallas as pl
from jax.experimental.pallas import tpu as pltpu
from jax.sharding import PartitionSpec as P

MESH = pl.DeviceIdType.MESH
F32, BF16 = jnp.float32, jnp.bfloat16
CI = 8
TY = 16


def dot(a, b):
    return jnp.dot(a, b, preferred_element_type=F32)


def exchange_kernel(R, C, u, a, b, bt, c, ct, d, h5, ubuf, sa, sb, tx1, rx1, tx2, rx2, tx3, rx3, tx4, dbuf,
                    usem, dsem, s1, r1, s2, r2, s3, r3, s4, r4, lsem):
    X, Y, Z = u.shape
    J, I = d.shape[1], d.shape[0]
    N = X
    n = I // CI
    me_r, me_c = lax.axis_index("row"), lax.axis_index("col")

    def row_peer(off):
        return lax.rem(me_r + off, R)

    def col_peer(off):
        return lax.rem(me_c + off, C)

    def load_u(t):
        return pltpu.make_async_copy(u.at[:, pl.ds(t * TY, TY), :], ubuf.at[t % 2], usem.at[t % 2])

    def load_d(k, slot):
        return pltpu.make_async_copy(d.at[pl.ds(k * CI, CI)], dbuf.at[slot], dsem.at[slot])

    load_u(0).start()
    load_u(1).start()
    load_d(0, 0).start()

    barrier = pltpu.get_barrier_semaphore()
    for off in range(1, R):
        pl.semaphore_signal(barrier, inc=1, device_id={"row": row_peer(off)}, device_id_type=MESH)
    for off in range(1, C):
        pl.semaphore_signal(barrier, inc=1, device_id={"col": col_peer(off)}, device_id_type=MESH)

    def send_row(k, y0, ny):
        for off in range(1, R):
            p = row_peer(off)
            pltpu.make_async_remote_copy(
                src_ref=tx1.at[pl.ds(p * I + k * CI, CI), pl.ds(y0, ny), :],
                dst_ref=rx1.at[k, :, pl.ds(pl.multiple_of(me_r * Y + y0, TY), ny), :],
                send_sem=s1, recv_sem=r1.at[k], device_id={"row": p}, device_id_type=MESH).start()

    def keep_row(k):
        y0 = pl.multiple_of(me_r * Y, Y)
        rx1[k, :, pl.ds(y0, Y), :] = tx1[pl.ds(me_r * I + k * CI, CI), :, :]

    for t in range(Y // TY):
        load_u(t).wait()
        slot = t % 2

        def spread(g, _):
            x0 = g * 32
            v = ubuf[slot, pl.ds(x0, 32)].astype(F32)
            for h in range(TY // 8):
                sa[h, pl.ds(pl.multiple_of(x0 * 8, 256), 256), :] = v[:, h * 8:(h + 1) * 8, :].reshape(256, Z)
            return 0

        lax.fori_loop(0, X // 32, spread, 0)
        if t + 2 < Y // TY:
            load_u(t + 2).start()
        for h in range(TY // 8):
            def pair(q, _):
                y = 2 * q
                rhs = jnp.concatenate(
                    [sa[h, pl.ds(y, X, stride=8), :].astype(BF16), sa[h, pl.ds(y + 1, X, stride=8), :].astype(BF16)], axis=1)
                res = dot(a[...], rhs)
                sb[h, pl.ds(y, N, stride=8), :] = res[:, :Z]
                sb[h, pl.ds(y + 1, N, stride=8), :] = res[:, Z:]
                return 0

            lax.fori_loop(0, 4, pair, 0)

        def gather(g, _):
            i0 = g * 32
            parts = [sb[h, pl.ds(pl.multiple_of(i0 * 8, 256), 256), :].reshape(32, 8, Z) for h in range(TY // 8)]
            tx1[pl.ds(i0, 32), pl.ds(t * TY, TY), :] = jnp.concatenate(parts, axis=1).astype(BF16)
            return 0

        lax.fori_loop(0, N // 32, gather, 0)
        if t == 0:
            pl.semaphore_wait(barrier, R - 1 + C - 1)
        send_row(0, t * TY, TY)

    def rest(k, _):
        send_row(k, 0, Y)
        return 0

    lax.fori_loop(1, n, rest, 0)

    def own(k, _):
        keep_row(k)
        return 0

    lax.fori_loop(0, n, own, 0)

    def wait_bytes(ref, sem):
        pltpu.make_async_copy(ref, ref, sem).wait()

    def step(k, _):
        @pl.when(k < n)
        def _():
            wait_bytes(rx1.at[k, pl.ds(0, CI * (R - 1) // R)], r1.at[k])
            slot = lax.rem(k, 2)

            @pl.when(k >= 2)
            def _():
                wait_bytes(tx2.at[slot, :, pl.ds(0, J * (C - 1)), :], s2.at[slot])

            def pair(q, _):
                i = 2 * q
                rhs = jnp.concatenate([rx1[k, i], rx1[k, i + 1]], axis=1)
                res = dot(b[...], rhs).astype(BF16)
                tx2[slot, i] = res[:, :Z]
                tx2[slot, i + 1] = res[:, Z:]
                return 0

            lax.fori_loop(0, CI // 2, pair, 0)
            for off in range(1, C):
                p = col_peer(off)
                pltpu.make_async_remote_copy(
                    src_ref=tx2.at[slot, :, pl.ds(pl.multiple_of(p * J, J), J), :], dst_ref=rx2.at[k, me_c],
                    send_sem=s2.at[slot], recv_sem=r2.at[k], device_id={"col": p}, device_id_type=MESH).start()
            rx2[k, me_c] = tx2[slot, :, pl.ds(pl.multiple_of(me_c * J, J), J), :]

        @pl.when(jnp.logical_and(k >= 1, k < n + 1))
        def _():
            m = k - 1
            slot = lax.rem(m, 2)

            @pl.when(m + 1 < n)
            def _():
                load_d(m + 1, 1 - slot).start()

            load_d(m, slot).wait()
            wait_bytes(rx2.at[m, pl.ds(0, C - 1)], r2.at[m])

            @pl.when(m >= 2)
            def _():
                wait_bytes(tx3.at[slot, pl.ds(0, C - 1)], s3.at[slot])

            def pair(q, _):
                i = 2 * q
                lhs = jnp.concatenate([rx2[m, e, pl.ds(i, 2)].reshape(2 * J, Z) for e in range(C)], axis=1)
                h3 = (dot(lhs, ct[...]) * dbuf[slot, pl.ds(i, 2)].reshape(2 * J, N)).astype(BF16)
                h4 = dot(h3, c[...]).astype(BF16)
                for e in range(C):
                    tx3[slot, e, pl.ds(i, 2)] = h4[:, e * Z:(e + 1) * Z].reshape(2, J, Z)
                return 0

            lax.fori_loop(0, CI // 2, pair, 0)
            for off in range(1, C):
                p = col_peer(off)
                pltpu.make_async_remote_copy(
                    src_ref=tx3.at[slot, p], dst_ref=rx3.at[m, :, pl.ds(pl.multiple_of(me_c * J, J), J), :],
                    send_sem=s3.at[slot], recv_sem=r3.at[m], device_id={"col": p}, device_id_type=MESH).start()
            rx3[m, :, pl.ds(pl.multiple_of(me_c * J, J), J), :] = tx3[slot, me_c]

        @pl.when(k >= 2)
        def _():
            m = k - 2
            slot = lax.rem(m, 2)
            wait_bytes(rx3.at[m, :, pl.ds(0, J * (C - 1)), :], r3.at[m])

            def own_copy(m, slot):
                return pltpu.make_async_copy(
                    tx4.at[slot, pl.ds(pl.multiple_of(me_r * Y, Y), Y)],
                    h5.at[:, pl.ds(pl.multiple_of(me_r * I + m * CI, CI), CI), :], lsem.at[slot])

            @pl.when(m >= 2)
            def _():
                wait_bytes(tx4.at[slot, pl.ds(0, Y * (R - 1))], s4.at[slot])
                own_copy(m - 2, slot).wait()

            def pair(q, _):
                i = 2 * q
                rhs = jnp.concatenate([rx3[m, i], rx3[m, i + 1]], axis=1)
                res = dot(bt[...], rhs)
                sa[0, pl.ds(i, N, stride=8), :] = res[:, :Z]
                sa[0, pl.ds(i + 1, N, stride=8), :] = res[:, Z:]
                return 0

            lax.fori_loop(0, CI // 2, pair, 0)

            def pack(g, _):
                y0 = g * 32
                tx4[slot, pl.ds(y0, 32)] = sa[0, pl.ds(pl.multiple_of(y0 * 8, 256), 256), :].reshape(32, 8, Z).astype(BF16)
                return 0

            lax.fori_loop(0, N // 32, pack, 0)
            for off in range(1, R):
                p = row_peer(off)
                pltpu.make_async_remote_copy(
                    src_ref=tx4.at[slot, pl.ds(pl.multiple_of(p * Y, Y), Y)],
                    dst_ref=h5.at[:, pl.ds(pl.multiple_of(me_r * I + m * CI, CI), CI), :],
                    send_sem=s4.at[slot], recv_sem=r4, device_id={"row": p}, device_id_type=MESH).start()
            own_copy(m, slot).start()

        return 0

    lax.fori_loop(0, n + 2, step, 0)

    wait_bytes(tx1.at[pl.ds(0, I * (R - 1))], s1)
    for m in (n - 2, n - 1):
        slot = m % 2
        wait_bytes(tx2.at[slot, :, pl.ds(0, J * (C - 1)), :], s2.at[slot])
        wait_bytes(tx3.at[slot, pl.ds(0, C - 1)], s3.at[slot])
        wait_bytes(tx4.at[slot, pl.ds(0, Y * (R - 1))], s4.at[slot])
        pltpu.make_async_copy(
            tx4.at[slot, pl.ds(0, Y)], h5.at[:, pl.ds(0, CI), :], lsem.at[slot]).wait()
    pltpu.make_async_copy(h5.at[:, pl.ds(0, I * (R - 1)), :], h5.at[:, pl.ds(0, I * (R - 1)), :], r4).wait()


def exchange(R, C, u, a, b, bt, c, ct, d):
    X, Y, Z = u.shape
    I, J, N = d.shape
    n = I // CI
    vm = pl.BlockSpec(memory_space=pltpu.VMEM)
    hb = pl.BlockSpec(memory_space=pl.ANY)
    DMA = pltpu.SemaphoreType.DMA
    return pl.pallas_call(
        functools.partial(exchange_kernel, R, C),
        name="exchange",
        out_shape=jax.ShapeDtypeStruct((Y, N, Z), BF16),
        in_specs=[hb, vm, vm, vm, vm, vm, hb],
        out_specs=hb,
        scratch_shapes=[
            pltpu.VMEM((2, X, TY, Z), BF16),
            pltpu.VMEM((TY // 8, X * 8, Z), F32),
            pltpu.VMEM((TY // 8, N * 8, Z), F32),
            pltpu.VMEM((N, Y, Z), BF16),
            pltpu.VMEM((n, CI, N, Z), BF16),
            pltpu.VMEM((2, CI, N, Z), BF16),
            pltpu.VMEM((n, C, CI, J, Z), BF16),
            pltpu.VMEM((2, C, CI, J, Z), BF16),
            pltpu.VMEM((n, CI, N, Z), BF16),
            pltpu.VMEM((2, N, CI, Z), BF16),
            pltpu.VMEM((2, CI, J, N), F32),
            DMA((2,)), DMA((2,)), DMA, DMA((n,)), DMA((2,)), DMA((n,)), DMA((2,)), DMA((n,)), DMA((2,)), DMA, DMA((2,)),
        ],
        compiler_params=pltpu.CompilerParams(
            collective_id=0, has_side_effects=True, vmem_limit_bytes=67043328),
    )(u, a, b, bt, c, ct, d)


def last_kernel(at, h, w):
    TYO = h.shape[0]
    Z = h.shape[2]
    flat = w.reshape(w.shape[0] * TYO, Z)
    X = w.shape[0]
    for q in range(TYO // 2):
        y = 2 * q
        res = dot(at[...], jnp.concatenate([h[y], h[y + 1]], axis=1))
        flat[pl.ds(y, X, stride=TYO), :] = res[:, :Z]
        flat[pl.ds(y + 1, X, stride=TYO), :] = res[:, Z:]


def last(at, h5):
    Y, N, Z = h5.shape
    X = at.shape[0]
    T = 8
    return pl.pallas_call(
        last_kernel,
        name="last",
        grid=(Y // T,),
        out_shape=jax.ShapeDtypeStruct((X, Y, Z), F32),
        in_specs=[pl.BlockSpec((X, N), lambda t: (0, 0)), pl.BlockSpec((T, N, Z), lambda t: (t, 0, 0))],
        out_specs=pl.BlockSpec((X, T, Z), lambda t: (0, t, 0)),
        compiler_params=pltpu.CompilerParams(vmem_limit_bytes=32 * 2**20),
    )(at, h5)


def solution(mesh):
    R, C = mesh.shape["row"], mesh.shape["col"]

    def local_apply(field_u, fac_a, fac_b, fac_c, diag_d):
        outs = []
        for e in range(field_u.shape[0]):
            h5 = exchange(R, C, field_u[e], fac_a, fac_b, fac_b.T, fac_c, fac_c.T, diag_d)
            outs.append(last(fac_a.T, h5))
        return jnp.stack(outs) if len(outs) > 1 else outs[0][None]

    spec = P("fields", None, "row", "col")
    fac = P("fields", None)
    return jax.shard_map(local_apply, mesh=mesh, in_specs=(spec, fac, fac, fac, P(("fields", "row"), "col", None)),
                         out_specs=spec, check_vma=False)
```

time: 668 us -> 248 us (0.37); the launches traced: 656 us -> 248 us
  blocking collectives: 401 us -> 0 us
  Pallas kernels: 0 us -> 237 us
  local copies, waits for them, and re-layouts: 152 us -> 10.7 us
  matrix products: 103 us -> 0 us
    all_to_all x4 -> x0, blocking collectives: 401 us -> none  [the longest x1 102 us: local_apply(): z_pencil = lax.all_to_all(stage_two, 'col', 2, 3, tiled=True)]
    pallas_call x0 -> x2, Pallas kernels: none -> 237 us  [the longest x1 228 us: exchange(): pl.pallas_call(functools.partial(exchange_kernel, R, C), name='exchange',...]
    dot_general x5 -> x0, matrix products: 103 us -> none  [the longest x1 41.8 us: local_apply(): jnp.einsum('ix,biyz->bxyz', fac_a, back_x, preferred_element_type=jnp.flo...]
    all_to_all x6 -> x0, local copies, waits for them, and re-layouts: 74.1 us -> none  [the longest x2 24.2 us: local_apply(): z_pencil = lax.all_to_all(stage_two, 'col', 2, 3, tiled=True)]
    convert_element_type x4 -> x0, local copies, waits for them, and re-layouts: 48 us -> none  [the longest x1 12.1 us: local_apply(): jnp.einsum('ix,bxyz->biyz', fac_a, field_u, preferred_element_type=jnp.fl...]
    transpose x1 -> x0, local copies, waits for them, and re-layouts: 16.5 us -> none  [local_apply(): jnp.einsum('ix,biyz->bxyz', fac_a, back_x, preferred_element_type=jnp.flo...]
    another operation x1 -> x0, local copies, waits for them, and re-layouts: 13.1 us -> none
    unnamed x6 -> x7, local copies, waits for them, and re-layouts: 0.01 us -> 10.7 us
where the time goes in v1:
time: 248 us
  Pallas kernels  237 us (96%)
  local copies, waits for them, and re-layouts  10.7 us (4%)
    pallas_call x1, Pallas kernels, exchange(): pl.pallas_call(functools.partial(exchange_kernel, R, C), name='exchange',...  228 us
    unnamed x7, local copies, waits for them, and re-layouts  10.7 us
    pallas_call x1, Pallas kernels, last(): pl.pallas_call(last_kernel, name='last', grid=(Y // T,), out_shape=jax.Sh...  9.17 us

profile of v1, /device:TPU:97, one launch (start us, length us, event | category | flops | bytes accessed | tf_op | source)
XLA Modules:
  0.0 247.6 jit_solution(13999686096564076938)
XLA Ops:
  0.0 2.0 copy.6
  2.0 2.1 copy.7
  4.2 2.1 copy.8
  6.3 227.7 %exchange.1.h = bf16[64,512,128]{2,1,0:T(8,128)(2,1)} custom-call(bf16[512,64,128]{2,1,0:T(8,128)(2,1)} %bitcast.6, bf16[512,512]{1,0:T(8,128)(2,1)} %a.1, bf16[512,512]{1,0:T(8,128)(2,1)} %b.1, bf16[512,512]{1,0:T(8,128)(2,1)} %bitcast.7, bf16[512,512]{1,0:T(8,128)(2,1)} %c.1, bf16[512,512]{1,0:T(8,128)(2,1)} %bitcast.8, f32[64,128,512]{2,1,0:T(8,128)} %d.1), custom_call_target="tpu_custom_call" | custom-call | tf_op jit(solution)/shard_map/exchange/pallas_call | solution.py:235
  234.0 0.0 copy-start
  234.0 3.4 %copy-done = bf16[64,512,128]{2,1,0:T(8,128)(2,1)S(1)} copy-done((bf16[64,512,128]{2,1,0:T(8,128)(2,1)S(1)}, bf16[64,512,128]{2,1,0:T(8,128)(2,1)}, u32[]{:S(2)}) %copy-start) | copy-done | bytes 8388632
  237.4 0.0 copy-start.1
  237.4 1.0 copy-done.1
  238.4 9.2 %last.1 = f32[512,64,128]{2,1,0:T(8,128)} custom-call(bf16[512,512]{1,0:T(8,128)(2,1)S(1)} %bitcast.5, bf16[64,512,128]{2,1,0:T(8,128)(2,1)S(1)} %copy-done), custom_call_target="tpu_custom_call" | custom-call | tf_op jit(solution)/shard_map/last/pallas_call | solution.py:276
Async XLA Ops:
  234.0 3.4 %copy-start = (bf16[64,512,128]{2,1,0:T(8,128)(2,1)S(1)}, bf16[64,512,128]{2,1,0:T(8,128)(2,1)}, u32[]{:S(2)}) copy-start(bf16[64,512,128]{2,1,0:T(8,128)(2,1)} %exchange.1.h) | copy-start | bytes 25165828
  237.4 1.0 copy-start.1

commit v2 on v1

v2 whole, which is shorter than its diff:
```python
import functools

import jax
import jax.numpy as jnp
from jax import lax
from jax.experimental import pallas as pl
from jax.experimental.pallas import tpu as pltpu
from jax.sharding import PartitionSpec as P

MESH = pl.DeviceIdType.MESH
F32, BF16 = jnp.float32, jnp.bfloat16
CI = 2
TY = 16
AHEAD = 4
EARLY = 2
LAG3, LAG5 = 1, 3
SLOTS = 4


def dot(a, b):
    return jnp.dot(a, b, preferred_element_type=F32)


def wait_bytes(ref, sem):
    pltpu.make_async_copy(ref, ref, sem).wait()


def exchange_kernel(R, C, u, a_hbm, b_hbm, c_hbm, d, h5, at_out, mats, ubuf, sa, sb, tx1, rx1, tx2, rx2, tx3, rx3, tx4,
                    dbuf, msem, usem, dsem, s1, r1, s2, r2, s3, r3, s4, r4, lsem, asem):
    X, Y, Z = u.shape
    I, J, N = d.shape
    n = I // CI
    a, b, c, at, bt, ct = (mats.at[e] for e in range(6))
    me_r, me_c = lax.axis_index("row"), lax.axis_index("col")

    def row_peer(off):
        return lax.rem(me_r + off, R)

    def col_peer(off):
        return lax.rem(me_c + off, C)

    def load_u(t):
        return pltpu.make_async_copy(u.at[:, pl.ds(t * TY, TY), :], ubuf.at[t % 2], usem.at[t % 2])

    def load_d(k):
        slot = lax.rem(k, SLOTS)
        return pltpu.make_async_copy(d.at[pl.ds(k * CI, CI)], dbuf.at[slot], dsem.at[slot])

    load_u(0).start()
    loads = [pltpu.make_async_copy(h, mats.at[e], msem.at[e]) for e, h in enumerate((a_hbm, b_hbm, c_hbm))]
    loads[0].start()
    load_u(1).start()
    for e in (1, 2):
        loads[e].start()

    barrier = pltpu.get_barrier_semaphore()
    for off in range(1, R):
        pl.semaphore_signal(barrier, inc=1, device_id={"row": row_peer(off)}, device_id_type=MESH)
    for off in range(1, C):
        pl.semaphore_signal(barrier, inc=1, device_id={"col": col_peer(off)}, device_id_type=MESH)

    def send_row(k, y0, ny):
        for off in range(1, R):
            p = row_peer(off)
            pltpu.make_async_remote_copy(
                src_ref=tx1.at[pl.ds(p * I + k * CI, CI), pl.ds(y0, ny), :],
                dst_ref=rx1.at[k, :, pl.ds(pl.multiple_of(me_r * Y + y0, TY), ny), :],
                send_sem=s1, recv_sem=r1.at[k], device_id={"row": p}, device_id_type=MESH).start()

    for t in range(Y // TY):
        load_u(t).wait()
        slot = t % 2

        def spread(g, _):
            x0 = g * 32
            v = ubuf[slot, pl.ds(x0, 32)].astype(F32)
            for h in range(TY // 8):
                sa[h, pl.ds(pl.multiple_of(x0 * 8, 256), 256), :] = v[:, h * 8:(h + 1) * 8, :].reshape(256, Z)
            return 0

        lax.fori_loop(0, X // 32, spread, 0)
        if t + 2 < Y // TY:
            load_u(t + 2).start()
        if t == 0:
            loads[0].wait()

        def tile(h, _):
            rhs = jnp.concatenate([sa[h, pl.ds(e, X, stride=8), :].astype(BF16) for e in range(8)], axis=1)
            res = dot(a[...], rhs)
            for e in range(8):
                sb[h, pl.ds(e, N, stride=8), :] = res[:, e * Z:(e + 1) * Z]
            return 0

        lax.fori_loop(0, TY // 8, tile, 0)

        def gather(g, _):
            i0 = g * 32
            parts = [sb[h, pl.ds(pl.multiple_of(i0 * 8, 256), 256), :].reshape(32, 8, Z) for h in range(TY // 8)]
            tx1[pl.ds(i0, 32), pl.ds(t * TY, TY), :] = jnp.concatenate(parts, axis=1).astype(BF16)
            return 0

        lax.fori_loop(0, N // 32, gather, 0)
        if t == 0:
            pl.semaphore_wait(barrier, R - 1 + C - 1)
        for k in range(EARLY):
            send_row(k, t * TY, TY)

    for k in range(EARLY, AHEAD):
        send_row(k, 0, Y)
    for k in range(LAG3 + 2):
        load_d(k).start()

    def own(k, _):
        rx1[k, :, pl.ds(pl.multiple_of(me_r * Y, Y), Y), :] = tx1[pl.ds(me_r * I + k * CI, CI), :, :]
        return 0

    lax.fori_loop(0, n, own, 0)
    loads[1].wait()
    loads[2].wait()
    for e in range(3):
        mats[3 + e] = mats[e].T
    save_at = pltpu.make_async_copy(at, at_out, asem)
    save_at.start()

    def own_copy(m, slot):
        return pltpu.make_async_copy(
            tx4.at[slot, :, pl.ds(pl.multiple_of(me_r * Y, Y), Y), :], h5.at[pl.ds(me_r * I + m * CI, CI)], lsem.at[slot])

    def free2(slot):
        wait_bytes(tx2.at[slot, :, pl.ds(0, J * (C - 1)), :], s2.at[slot])

    def free3(slot):
        wait_bytes(tx3.at[slot, pl.ds(0, C - 1)], s3.at[slot])

    def free4(m, slot):
        wait_bytes(tx4.at[slot, :, pl.ds(0, Y * (R - 1)), :], s4.at[slot])
        own_copy(m, slot).wait()

    def step(k, _):
        @pl.when(k + AHEAD < n)
        def _():
            send_row(k + AHEAD, 0, Y)

        @pl.when(k < n)
        def _():
            slot = lax.rem(k, SLOTS)
            wait_bytes(rx1.at[k, :, pl.ds(0, Y * (R - 1)), :], r1.at[k])

            @pl.when(k >= SLOTS)
            def _():
                free2(slot)

            res = dot(b[...], jnp.concatenate([rx1[k, i] for i in range(CI)], axis=1)).astype(BF16)
            for i in range(CI):
                tx2[slot, i] = res[:, i * Z:(i + 1) * Z]
            for off in (2, 1, 3):
                p = col_peer(off)
                pltpu.make_async_remote_copy(
                    src_ref=tx2.at[slot, :, pl.ds(pl.multiple_of(p * J, J), J), :], dst_ref=rx2.at[k, me_c],
                    send_sem=s2.at[slot], recv_sem=r2.at[k], device_id={"col": p}, device_id_type=MESH).start()
            rx2[k, me_c] = tx2[slot, :, pl.ds(pl.multiple_of(me_c * J, J), J), :]

        m = k - LAG3

        @pl.when(jnp.logical_and(m >= 0, m < n))
        def _():
            slot = lax.rem(m, SLOTS)

            @pl.when(m + LAG3 + 2 < n)
            def _():
                load_d(m + LAG3 + 2).start()

            load_d(m).wait()
            wait_bytes(rx2.at[m, pl.ds(0, C - 1)], r2.at[m])

            @pl.when(m >= SLOTS)
            def _():
                free3(slot)

            lhs = jnp.concatenate([rx2[m, e].reshape(CI * J, Z) for e in range(C)], axis=1)
            h3 = (dot(lhs, ct[...]) * dbuf[slot].reshape(CI * J, N)).astype(BF16)
            h4 = dot(h3, c[...]).astype(BF16)
            for e in range(C):
                tx3[slot, e] = h4[:, e * Z:(e + 1) * Z].reshape(CI, J, Z)
            for off in (2, 1, 3):
                p = col_peer(off)
                pltpu.make_async_remote_copy(
                    src_ref=tx3.at[slot, p], dst_ref=rx3.at[m, :, pl.ds(pl.multiple_of(me_c * J, J), J), :],
                    send_sem=s3.at[slot], recv_sem=r3.at[m], device_id={"col": p}, device_id_type=MESH).start()
            rx3[m, :, pl.ds(pl.multiple_of(me_c * J, J), J), :] = tx3[slot, me_c]

        o = k - LAG5

        @pl.when(o >= 0)
        def _():
            slot = lax.rem(o, SLOTS)
            wait_bytes(rx3.at[o, :, pl.ds(0, J * (C - 1)), :], r3.at[o])

            @pl.when(o >= SLOTS)
            def _():
                free4(o - SLOTS, slot)

            res = dot(bt[...], jnp.concatenate([rx3[o, i] for i in range(CI)], axis=1)).astype(BF16)
            for i in range(CI):
                tx4[slot, i] = res[:, i * Z:(i + 1) * Z]
            for off in (4, 5, 3, 2, 6, 7, 1):
                p = row_peer(off)
                pltpu.make_async_remote_copy(
                    src_ref=tx4.at[slot, :, pl.ds(pl.multiple_of(p * Y, Y), Y), :],
                    dst_ref=h5.at[pl.ds(me_r * I + o * CI, CI)],
                    send_sem=s4.at[slot], recv_sem=r4, device_id={"row": p}, device_id_type=MESH).start()
            own_copy(o, slot).start()

        return 0

    lax.fori_loop(0, n + LAG5, step, 0)

    save_at.wait()
    wait_bytes(tx1.at[pl.ds(0, I * (R - 1))], s1)
    for m in range(n - SLOTS, n):
        free2(m % SLOTS)
        free3(m % SLOTS)
        free4(m, m % SLOTS)
    wait_bytes(h5.at[pl.ds(0, I * (R - 1))], r4)


def exchange(R, C, u, a, b, c, d):
    X, Y, Z = u.shape
    I, J, N = d.shape
    n = I // CI
    hb = pl.BlockSpec(memory_space=pl.ANY)
    DMA = pltpu.SemaphoreType.DMA
    return pl.pallas_call(
        functools.partial(exchange_kernel, R, C),
        name="exchange",
        out_shape=(jax.ShapeDtypeStruct((N, Y, Z), BF16), jax.ShapeDtypeStruct((X, N), BF16)),
        in_specs=[hb] * 5,
        out_specs=(hb, hb),
        scratch_shapes=[
            pltpu.VMEM((6, N, X), BF16),
            pltpu.VMEM((2, X, TY, Z), BF16),
            pltpu.VMEM((TY // 8, X * 8, Z), F32),
            pltpu.VMEM((TY // 8, N * 8, Z), F32),
            pltpu.VMEM((N, Y, Z), BF16),
            pltpu.VMEM((n, CI, N, Z), BF16),
            pltpu.VMEM((SLOTS, CI, N, Z), BF16),
            pltpu.VMEM((n, C, CI, J, Z), BF16),
            pltpu.VMEM((SLOTS, C, CI, J, Z), BF16),
            pltpu.VMEM((n, CI, N, Z), BF16),
            pltpu.VMEM((SLOTS, CI, N, Z), BF16),
            pltpu.VMEM((SLOTS, CI, J, N), F32),
            DMA((3,)), DMA((2,)), DMA((SLOTS,)), DMA, DMA((n,)), DMA((SLOTS,)), DMA((n,)), DMA((SLOTS,)), DMA((n,)),
            DMA((SLOTS,)), DMA, DMA((SLOTS,)), DMA,
        ],
        compiler_params=pltpu.CompilerParams(
            collective_id=0, has_side_effects=True, vmem_limit_bytes=67043328),
    )(u, a, b, c, d)


def last_kernel(at, h, w, sa):
    N, T, Z = h.shape
    X = w.shape[0]

    def spread(g, _):
        i0 = g * 32
        sa[pl.ds(pl.multiple_of(i0 * T, 32 * T), 32 * T), :] = h[pl.ds(i0, 32)].astype(F32).reshape(32 * T, Z)
        return 0

    lax.fori_loop(0, N // 32, spread, 0)
    rhs = jnp.concatenate([sa[pl.ds(e, N, stride=T), :].astype(BF16) for e in range(T)], axis=1)
    res = dot(at[...], rhs)
    flat = w.reshape(X * T, Z)
    for e in range(T):
        flat[pl.ds(e, X, stride=T), :] = res[:, e * Z:(e + 1) * Z]


def last(at, h5):
    N, Y, Z = h5.shape
    X = at.shape[0]
    T = 8
    return pl.pallas_call(
        last_kernel,
        name="last",
        grid=(Y // T,),
        out_shape=jax.ShapeDtypeStruct((X, Y, Z), F32),
        in_specs=[pl.BlockSpec((X, N), lambda t: (0, 0)), pl.BlockSpec((N, T, Z), lambda t: (0, t, 0))],
        out_specs=pl.BlockSpec((X, T, Z), lambda t: (0, t, 0)),
        scratch_shapes=[pltpu.VMEM((N * T, Z), F32)],
        compiler_params=pltpu.CompilerParams(vmem_limit_bytes=62 * 2**20),
    )(at, h5)


def solution(mesh):
    R, C = mesh.shape["row"], mesh.shape["col"]

    def local_apply(field_u, fac_a, fac_b, fac_c, diag_d):
        outs = []
        for e in range(field_u.shape[0]):
            h5, at = exchange(R, C, field_u[e], fac_a, fac_b, fac_c, diag_d)
            outs.append(last(at, h5))
        return jnp.stack(outs) if len(outs) > 1 else outs[0][None]

    spec = P("fields", None, "row", "col")
    fac = P("fields", None)
    return jax.shard_map(local_apply, mesh=mesh, in_specs=(spec, fac, fac, fac, P(("fields", "row"), "col", None)),
                         out_specs=spec, check_vma=False)
```

time: 248 us -> 226 us (0.911)
  Pallas kernels: 237 us -> 226 us
  local copies, waits for them, and re-layouts: 10.7 us -> 0 us
    pallas_call x1, Pallas kernels: 228 us -> 211 us  [exchange(): pl.pallas_call(functools.partial(exchange_kernel, R, C), name='exchange',...]
    unnamed x7 -> x0, local copies, waits for them, and re-layouts: 10.7 us -> none
    pallas_call x1, Pallas kernels: 9.17 us -> 14.3 us  [last(): pl.pallas_call(last_kernel, name='last', grid=(Y // T,), out_shape=jax.Sh...]
where the time goes in v2:
time: 226 us
  Pallas kernels  226 us (100%)
    pallas_call x1, Pallas kernels, exchange(): pl.pallas_call(functools.partial(exchange_kernel, R, C), name='exchange',...  211 us
    pallas_call x1, Pallas kernels, last(): pl.pallas_call(last_kernel, name='last', grid=(Y // T,), out_shape=jax.Sh...  14.3 us

profile of v2, /device:TPU:97, one launch (start us, length us, event | category | flops | bytes accessed | tf_op | source)
XLA Modules:
  0.0 225.8 jit_solution(2572927142401213224)
XLA Ops:
  0.0 211.5 %exchange.1 = (bf16[512,64,128]{2,1,0:T(8,128)(2,1)}, bf16[512,512]{1,0:T(8,128)(2,1)}) custom-call(bf16[512,64,128]{2,1,0:T(8,128)(2,1)} %bitcast.2, bf16[512,512]{1,0:T(8,128)(2,1)} %a_hbm.1, bf16[512,512]{1,0:T(8,128)(2,1)} %b_hbm.1, bf16[512,512]{1,0:T(8,128)(2,1)} %c_hbm.1, f32[64,128,512]{2,1,0:T(8,128)} %d.1), custom_call_target="tpu_custom_call" | custom-call | tf_op jit(solution)/shard_map/exchange/pallas_call | solution.py:233
  211.5 14.3 %last.1 = f32[512,64,128]{2,1,0:T(8,128)} custom-call(bf16[512,512]{1,0:T(8,128)(2,1)} %get-tuple-element.7.at, bf16[512,64,128]{2,1,0:T(8,128)(2,1)} %get-tuple-element.8.h), custom_call_target="tpu_custom_call" | custom-call | tf_op jit(solution)/shard_map/last/pallas_call | solution.py:281

commit v3 on v2

--- a/solution.py
+++ b/solution.py
@@ -11,6 +11,7 @@
 F32, BF16 = jnp.float32, jnp.bfloat16
 CI = 2
 TY = 16
+GI = 8
 AHEAD = 4
 EARLY = 2
 LAG3, LAG5 = 1, 3
@@ -25,8 +26,8 @@
     pltpu.make_async_copy(ref, ref, sem).wait()
 
 
-def exchange_kernel(R, C, u, a_hbm, b_hbm, c_hbm, d, h5, at_out, mats, ubuf, sa, sb, tx1, rx1, tx2, rx2, tx3, rx3, tx4,
-                    dbuf, msem, usem, dsem, s1, r1, s2, r2, s3, r3, s4, r4, lsem, asem):
+def exchange_kernel(R, C, u, a_hbm, b_hbm, c_hbm, d, h5, h5b, at_out, mats, ubuf, u2, sa, sb, tx1, rx1, tx2, rx2, tx3, rx3,
+                    tx4, tx4b, dbuf, msem, usem, dsem, s1, r1, s2, r2, s3, r3, s4, r4, lsem, s5, r5, lsem5, asem):
     X, Y, Z = u.shape
     I, J, N = d.shape
     n = I // CI
@@ -67,6 +68,30 @@
                 dst_ref=rx1.at[k, :, pl.ds(pl.multiple_of(me_r * Y + y0, TY), ny), :],
                 send_sem=s1, recv_sem=r1.at[k], device_id={"row": p}, device_id_type=MESH).start()
 
+    H = I // 2
+
+    def project(half, h, rhs):
+        res = dot(jnp.concatenate([a[pl.ds(e * I + half * H, H), :] for e in range(R)], axis=0), rhs)
+        for e in range(8):
+            sb[h, pl.ds(e, R * H, stride=8), :] = res[:, e * Z:(e + 1) * Z]
+
+    def gather(half, t):
+        def body(e, _):
+            parts = [sb[h, pl.ds(pl.multiple_of(e * H * 8, H * 8), H * 8), :].reshape(H, 8, Z) for h in range(TY // 8)]
+            tx1[pl.ds(e * I + half * H, H), pl.ds(pl.multiple_of(t * TY, TY), TY), :] = (
+                jnp.concatenate(parts, axis=1).astype(BF16))
+            return 0
+
+        lax.fori_loop(0, R, body, 0)
+
+    def second(t):
+        def body(h, _):
+            project(1, h, u2[t * (TY // 8) + h])
+            return 0
+
+        lax.fori_loop(0, TY // 8, body, 0)
+        gather(1, t)
+
     for t in range(Y // TY):
         load_u(t).wait()
         slot = t % 2
@@ -86,20 +111,12 @@
 
         def tile(h, _):
             rhs = jnp.concatenate([sa[h, pl.ds(e, X, stride=8), :].astype(BF16) for e in range(8)], axis=1)
-            res = dot(a[...], rhs)
-            for e in range(8):
-                sb[h, pl.ds(e, N, stride=8), :] = res[:, e * Z:(e + 1) * Z]
+            u2[t * (TY // 8) + h] = rhs
+            project(0, h, rhs)
             return 0
 
         lax.fori_loop(0, TY // 8, tile, 0)
-
-        def gather(g, _):
-            i0 = g * 32
-            parts = [sb[h, pl.ds(pl.multiple_of(i0 * 8, 256), 256), :].reshape(32, 8, Z) for h in range(TY // 8)]
-            tx1[pl.ds(i0, 32), pl.ds(t * TY, TY), :] = jnp.concatenate(parts, axis=1).astype(BF16)
-            return 0
-
-        lax.fori_loop(0, N // 32, gather, 0)
+        gather(0, t)
         if t == 0:
             pl.semaphore_wait(barrier, R - 1 + C - 1)
         for k in range(EARLY):
@@ -110,21 +127,29 @@
     for k in range(LAG3 + 2):
         load_d(k).start()
 
-    def own(k, _):
-        rx1[k, :, pl.ds(pl.multiple_of(me_r * Y, Y), Y), :] = tx1[pl.ds(me_r * I + k * CI, CI), :, :]
-        return 0
-
-    lax.fori_loop(0, n, own, 0)
+    second(0)
     loads[1].wait()
     loads[2].wait()
-    for e in range(3):
+    af = a[...].astype(F32)
+    keep = I - GI
+    order = [af[e * I:e * I + keep] for e in range(R)] + [af[e * I + keep:(e + 1) * I] for e in range(R)]
+    mats[3] = jnp.concatenate(order, axis=0).T.astype(BF16)
+    for e in (1, 2):
         mats[3 + e] = mats[e].T
     save_at = pltpu.make_async_copy(at, at_out, asem)
     save_at.start()
 
-    def own_copy(m, slot):
+    my_y = pl.ds(pl.multiple_of(me_r * Y, Y), Y)
+
+    def to_h5(g):
+        return h5.at[:, pl.ds(pl.multiple_of(me_r * keep + g * GI, GI), GI), :]
+
+    def own_copy(g, slot):
+        return pltpu.make_async_copy(tx4.at[slot, my_y], to_h5(g), lsem.at[slot])
+
+    def own_copy_b(q):
         return pltpu.make_async_copy(
-            tx4.at[slot, :, pl.ds(pl.multiple_of(me_r * Y, Y), Y), :], h5.at[pl.ds(me_r * I + m * CI, CI)], lsem.at[slot])
+            tx4b.at[q, :, my_y, :], h5b.at[pl.ds(me_r * GI + q * CI, CI)], lsem5.at[q])
 
     def free2(slot):
         wait_bytes(tx2.at[slot, :, pl.ds(0, J * (C - 1)), :], s2.at[slot])
@@ -132,9 +157,11 @@
     def free3(slot):
         wait_bytes(tx3.at[slot, pl.ds(0, C - 1)], s3.at[slot])
 
-    def free4(m, slot):
-        wait_bytes(tx4.at[slot, :, pl.ds(0, Y * (R - 1)), :], s4.at[slot])
-        own_copy(m, slot).wait()
+    def free4(g, slot):
+        wait_bytes(tx4.at[slot, pl.ds(0, Y * (R - 1))], s4.at[slot])
+        own_copy(g, slot).wait()
+
+    per = GI // CI
 
     def step(k, _):
         @pl.when(k + AHEAD < n)
@@ -144,6 +171,7 @@
         @pl.when(k < n)
         def _():
             slot = lax.rem(k, SLOTS)
+            rx1[k, :, my_y, :] = tx1[pl.ds(me_r * I + k * CI, CI), :, :]
             wait_bytes(rx1.at[k, :, pl.ds(0, Y * (R - 1)), :], r1.at[k])
 
             @pl.when(k >= SLOTS)
@@ -193,23 +221,51 @@
 
         @pl.when(o >= 0)
         def _():
-            slot = lax.rem(o, SLOTS)
             wait_bytes(rx3.at[o, :, pl.ds(0, J * (C - 1)), :], r3.at[o])
-
-            @pl.when(o >= SLOTS)
-            def _():
-                free4(o - SLOTS, slot)
-
-            res = dot(bt[...], jnp.concatenate([rx3[o, i] for i in range(CI)], axis=1)).astype(BF16)
-            for i in range(CI):
-                tx4[slot, i] = res[:, i * Z:(i + 1) * Z]
-            for off in (4, 5, 3, 2, 6, 7, 1):
-                p = row_peer(off)
-                pltpu.make_async_remote_copy(
-                    src_ref=tx4.at[slot, :, pl.ds(pl.multiple_of(p * Y, Y), Y), :],
-                    dst_ref=h5.at[pl.ds(me_r * I + o * CI, CI)],
-                    send_sem=s4.at[slot], recv_sem=r4, device_id={"row": p}, device_id_type=MESH).start()
-            own_copy(o, slot).start()
+            res = dot(bt[...], jnp.concatenate([rx3[o, i] for i in range(CI)], axis=1))
+            g, q = lax.div(o, per), lax.rem(o, per)
+            slot = lax.rem(g, 2)
+
+            @pl.when(o < n - per)
+            def _():
+                for i in range(CI):
+                    sa[0, pl.ds(q * CI + i, N, stride=GI), :] = res[:, i * Z:(i + 1) * Z]
+
+            @pl.when(jnp.logical_and(o < n - per, q == per - 1))
+            def _():
+                @pl.when(g >= 2)
+                def _():
+                    free4(g - 2, slot)
+
+                def pack(e, _):
+                    y0 = e * 32
+                    tx4[slot, pl.ds(y0, 32)] = (
+                        sa[0, pl.ds(pl.multiple_of(y0 * GI, 32 * GI), 32 * GI), :].reshape(32, GI, Z).astype(BF16))
+                    return 0
+
+                lax.fori_loop(0, N // 32, pack, 0)
+                for off in (4, 5, 3, 2, 6, 7, 1):
+                    p = row_peer(off)
+                    pltpu.make_async_remote_copy(
+                        src_ref=tx4.at[slot, pl.ds(pl.multiple_of(p * Y, Y), Y)], dst_ref=to_h5(g),
+                        send_sem=s4.at[slot], recv_sem=r4, device_id={"row": p}, device_id_type=MESH).start()
+                own_copy(g, slot).start()
+
+            @pl.when(o >= n - per)
+            def _():
+                for i in range(CI):
+                    tx4b[q, i] = res[:, i * Z:(i + 1) * Z].astype(BF16)
+                for off in (4, 5, 3, 2, 6, 7, 1):
+                    p = row_peer(off)
+                    pltpu.make_async_remote_copy(
+                        src_ref=tx4b.at[q, :, pl.ds(pl.multiple_of(p * Y, Y), Y), :],
+                        dst_ref=h5b.at[pl.ds(me_r * GI + q * CI, CI)],
+                        send_sem=s5, recv_sem=r5, device_id={"row": p}, device_id_type=MESH).start()
+                own_copy_b(q).start()
+
+        @pl.when(k < Y // TY - 1)
+        def _():
+            second(k + 1)
 
         return 0
 
@@ -220,8 +276,14 @@
     for m in range(n - SLOTS, n):
         free2(m % SLOTS)
         free3(m % SLOTS)
-        free4(m, m % SLOTS)
-    wait_bytes(h5.at[pl.ds(0, I * (R - 1))], r4)
+    groups = I // GI - 1
+    for g in (groups - 2, groups - 1):
+        free4(g, g % 2)
+    for q in range(per):
+        own_copy_b(q).wait()
+    wait_bytes(tx4b.at[:, :, pl.ds(0, Y * (R - 1)), :], s5)
+    wait_bytes(h5.at[:, pl.ds(0, keep * (R - 1)), :], r4)
+    wait_bytes(h5b.at[pl.ds(0, GI * (R - 1))], r5)
 
 
 def exchange(R, C, u, a, b, c, d):
@@ -233,61 +295,60 @@
     return pl.pallas_call(
         functools.partial(exchange_kernel, R, C),
         name="exchange",
-        out_shape=(jax.ShapeDtypeStruct((N, Y, Z), BF16), jax.ShapeDtypeStruct((X, N), BF16)),
+        out_shape=(jax.ShapeDtypeStruct((Y, N - R * GI, Z), BF16), jax.ShapeDtypeStruct((R * GI, Y, Z), BF16),
+                   jax.ShapeDtypeStruct((X, N), BF16)),
         in_specs=[hb] * 5,
-        out_specs=(hb, hb),
+        out_specs=(hb, hb, hb),
         scratch_shapes=[
             pltpu.VMEM((6, N, X), BF16),
             pltpu.VMEM((2, X, TY, Z), BF16),
+            pltpu.VMEM((Y // 8, X, 8 * Z), BF16),
             pltpu.VMEM((TY // 8, X * 8, Z), F32),
-            pltpu.VMEM((TY // 8, N * 8, Z), F32),
+            pltpu.VMEM((TY // 8, N // 2 * 8, Z), F32),
             pltpu.VMEM((N, Y, Z), BF16),
             pltpu.VMEM((n, CI, N, Z), BF16),
             pltpu.VMEM((SLOTS, CI, N, Z), BF16),
             pltpu.VMEM((n, C, CI, J, Z), BF16),
             pltpu.VMEM((SLOTS, C, CI, J, Z), BF16),
             pltpu.VMEM((n, CI, N, Z), BF16),
-            pltpu.VMEM((SLOTS, CI, N, Z), BF16),
+            pltpu.VMEM((2, N, GI, Z), BF16),
+            pltpu.VMEM((GI // CI, CI, N, Z), BF16),
             pltpu.VMEM((SLOTS, CI, J, N), F32),
             DMA((3,)), DMA((2,)), DMA((SLOTS,)), DMA, DMA((n,)), DMA((SLOTS,)), DMA((n,)), DMA((SLOTS,)), DMA((n,)),
-            DMA((SLOTS,)), DMA, DMA((SLOTS,)), DMA,
+            DMA((2,)), DMA, DMA((2,)), DMA, DMA, DMA((GI // CI,)), DMA,
         ],
         compiler_params=pltpu.CompilerParams(
             collective_id=0, has_side_effects=True, vmem_limit_bytes=67043328),
     )(u, a, b, c, d)
 
 
-def last_kernel(at, h, w, sa):
-    N, T, Z = h.shape
-    X = w.shape[0]
-
-    def spread(g, _):
-        i0 = g * 32
-        sa[pl.ds(pl.multiple_of(i0 * T, 32 * T), 32 * T), :] = h[pl.ds(i0, 32)].astype(F32).reshape(32 * T, Z)
-        return 0
-
-    lax.fori_loop(0, N // 32, spread, 0)
-    rhs = jnp.concatenate([sa[pl.ds(e, N, stride=T), :].astype(BF16) for e in range(T)], axis=1)
+def last_kernel(at, h, hb, w, sc):
+    T, K, Z = h.shape
+    Kb, X = hb.shape[0], w.shape[0]
+    sc[...] = hb[...].astype(F32).reshape(Kb * T, Z)
+    rhs = jnp.concatenate(
+        [jnp.concatenate([h[e], sc[pl.ds(e, Kb, stride=T), :].astype(BF16)], axis=0) for e in range(T)], axis=1)
     res = dot(at[...], rhs)
     flat = w.reshape(X * T, Z)
     for e in range(T):
         flat[pl.ds(e, X, stride=T), :] = res[:, e * Z:(e + 1) * Z]
 
 
-def last(at, h5):
-    N, Y, Z = h5.shape
-    X = at.shape[0]
+def last(at, h, hb):
+    Y, K, Z = h.shape
+    Kb, X = hb.shape[0], at.shape[0]
     T = 8
     return pl.pallas_call(
         last_kernel,
         name="last",
         grid=(Y // T,),
         out_shape=jax.ShapeDtypeStruct((X, Y, Z), F32),
-        in_specs=[pl.BlockSpec((X, N), lambda t: (0, 0)), pl.BlockSpec((N, T, Z), lambda t: (0, t, 0))],
+        in_specs=[pl.BlockSpec((X, K + Kb), lambda t: (0, 0)), pl.BlockSpec((T, K, Z), lambda t: (t, 0, 0)),
+                  pl.BlockSpec((Kb, T, Z), lambda t: (0, t, 0))],
         out_specs=pl.BlockSpec((X, T, Z), lambda t: (0, t, 0)),
-        scratch_shapes=[pltpu.VMEM((N * T, Z), F32)],
+        scratch_shapes=[pltpu.VMEM((Kb * T, Z), F32)],
         compiler_params=pltpu.CompilerParams(vmem_limit_bytes=62 * 2**20),
-    )(at, h5)
+    )(at, h, hb)
 
 
 def solution(mesh):
@@ -296,8 +357,8 @@
     def local_apply(field_u, fac_a, fac_b, fac_c, diag_d):
         outs = []
         for e in range(field_u.shape[0]):
-            h5, at = exchange(R, C, field_u[e], fac_a, fac_b, fac_c, diag_d)
-            outs.append(last(at, h5))
+            h5, h5b, at = exchange(R, C, field_u[e], fac_a, fac_b, fac_c, diag_d)
+            outs.append(last(at, h5, h5b))
         return jnp.stack(outs) if len(outs) > 1 else outs[0][None]
 
     spec = P("fields", None, "row", "col")

time: 226 us -> 225 us (level)
  no operation moved by 1% of the time
where the time goes in v3:
time: 225 us
  Pallas kernels  225 us (100%)
    pallas_call x1, Pallas kernels, exchange(): pl.pallas_call(functools.partial(exchange_kernel, R, C), name='exchange',...  211 us
    pallas_call x1, Pallas kernels, last(): pl.pallas_call(last_kernel, name='last', grid=(Y // T,), out_shape=jax.Sh...  13.1 us

profile of v3, /device:TPU:97, one launch (start us, length us, event | category | flops | bytes accessed | tf_op | source)
XLA Modules:
  0.0 224.5 jit_solution(9087334544426686978)
XLA Ops:
  0.0 211.5 %exchange.1 = (bf16[64,448,128]{2,1,0:T(8,128)(2,1)}, bf16[64,64,128]{2,1,0:T(8,128)(2,1)}, bf16[512,512]{1,0:T(8,128)(2,1)}) custom-call(bf16[512,64,128]{2,1,0:T(8,128)(2,1)} %bitcast.2, bf16[512,512]{1,0:T(8,128)(2,1)} %a_hbm.1, bf16[512,512]{1,0:T(8,128)(2,1)} %b_hbm.1, bf16[512,512]{1,0:T(8,128)(2,1)} %c_hbm.1, f32[64,128,512]{2,1,0:T(8,128)} %d.1), custom_call_target="tpu_custom_call" | custom-call | tf_op jit(solution)/shard_map/exchange/pallas_call | solution.py:295
  211.5 13.1 %last.1 = f32[512,64,128]{2,1,0:T(8,128)} custom-call(bf16[512,512]{1,0:T(8,128)(2,1)} %get-tuple-element.8.at, bf16[64,448,128]{2,1,0:T(8,128)(2,1)} %get-tuple-element.9.h, bf16[64,64,128]{2,1,0:T(8,128)(2,1)} %get-tuple-element.10.hb), custom_call_target="tpu_custom_call" | custom-call | tf_op jit(solution)/shard_map/last/pallas_call | solution.py:341

commit v4 on v3

--- a/solution.py
+++ b/solution.py
@@ -11,6 +11,7 @@
 F32, BF16 = jnp.float32, jnp.bfloat16
 CI = 2
 TY = 16
+PITCH = 9
 GI = 8
 AHEAD = 4
 EARLY = 2
@@ -26,12 +27,12 @@
     pltpu.make_async_copy(ref, ref, sem).wait()
 
 
-def exchange_kernel(R, C, u, a_hbm, b_hbm, c_hbm, d, h5, h5b, at_out, mats, ubuf, u2, sa, sb, tx1, rx1, tx2, rx2, tx3, rx3,
-                    tx4, tx4b, dbuf, msem, usem, dsem, s1, r1, s2, r2, s3, r3, s4, r4, lsem, s5, r5, lsem5, asem):
+def exchange_kernel(R, C, u, a_hbm, b_hbm, c_hbm, d, h5, h5b, at_out, mats, ubuf, sa, sb, tx1, rx1, tx2, rx2, tx3, rx3,
+                    tx4, tx4b, dbuf, msem, usem, dsem, s1, r1, s2, r2, s3, r3, s4, r4, s5, r5):
     X, Y, Z = u.shape
     I, J, N = d.shape
     n = I // CI
-    a, b, c, at, bt, ct = (mats.at[e] for e in range(6))
+    a, b, c, bt, ct = (mats.at[e] for e in range(5))
     me_r, me_c = lax.axis_index("row"), lax.axis_index("col")
 
     def row_peer(off):
@@ -65,7 +66,7 @@
             p = row_peer(off)
             pltpu.make_async_remote_copy(
                 src_ref=tx1.at[pl.ds(p * I + k * CI, CI), pl.ds(y0, ny), :],
-                dst_ref=rx1.at[k, :, pl.ds(pl.multiple_of(me_r * Y + y0, TY), ny), :],
+                dst_ref=rx1.at[pl.ds(k * CI, CI), pl.ds(pl.multiple_of(me_r * Y + y0, TY), ny), :],
                 send_sem=s1, recv_sem=r1.at[k], device_id={"row": p}, device_id_type=MESH).start()
 
     H = I // 2
@@ -73,20 +74,25 @@
     def project(half, h, rhs):
         res = dot(jnp.concatenate([a[pl.ds(e * I + half * H, H), :] for e in range(R)], axis=0), rhs)
         for e in range(8):
-            sb[h, pl.ds(e, R * H, stride=8), :] = res[:, e * Z:(e + 1) * Z]
+            sb[h, pl.ds(e, R * H, stride=PITCH), :] = res[:, e * Z:(e + 1) * Z]
 
     def gather(half, t):
         def body(e, _):
-            parts = [sb[h, pl.ds(pl.multiple_of(e * H * 8, H * 8), H * 8), :].reshape(H, 8, Z) for h in range(TY // 8)]
-            tx1[pl.ds(e * I + half * H, H), pl.ds(pl.multiple_of(t * TY, TY), TY), :] = (
-                jnp.concatenate(parts, axis=1).astype(BF16))
+            for i in range(H):
+                row = (e * H + i) * PITCH
+                parts = [sb[h, pl.ds(row, 8), :] for h in range(TY // 8)]
+                tx1[e * I + half * H + i, pl.ds(t * TY, TY), :] = jnp.concatenate(parts, axis=0).astype(BF16)
             return 0
 
         lax.fori_loop(0, R, body, 0)
+
+    def kept(t, h, e):
+        ref = rx3 if t < Y // TY // 2 else rx1
+        return ref.at[I // 2 + (t % (Y // TY // 2)) * TY + h * 8 + e]
 
     def second(t):
         def body(h, _):
-            project(1, h, u2[t * (TY // 8) + h])
+            project(1, h, jnp.concatenate([kept(t, h, e)[...] for e in range(8)], axis=1))
             return 0
 
         lax.fori_loop(0, TY // 8, body, 0)
@@ -99,8 +105,9 @@
         def spread(g, _):
             x0 = g * 32
             v = ubuf[slot, pl.ds(x0, 32)].astype(F32)
-            for h in range(TY // 8):
-                sa[h, pl.ds(pl.multiple_of(x0 * 8, 256), 256), :] = v[:, h * 8:(h + 1) * 8, :].reshape(256, Z)
+            for x in range(32):
+                for h in range(TY // 8):
+                    sa[h, pl.ds((x0 + x) * PITCH, 8), :] = v[x, h * 8:(h + 1) * 8, :]
             return 0
 
         lax.fori_loop(0, X // 32, spread, 0)
@@ -110,9 +117,10 @@
             loads[0].wait()
 
         def tile(h, _):
-            rhs = jnp.concatenate([sa[h, pl.ds(e, X, stride=8), :].astype(BF16) for e in range(8)], axis=1)
-            u2[t * (TY // 8) + h] = rhs
-            project(0, h, rhs)
+            cols = [sa[h, pl.ds(e, X, stride=PITCH), :].astype(BF16) for e in range(8)]
+            for e in range(8):
+                kept(t, h, e)[...] = cols[e]
+            project(0, h, jnp.concatenate(cols, axis=1))
             return 0
 
         lax.fori_loop(0, TY // 8, tile, 0)
@@ -133,24 +141,15 @@
     af = a[...].astype(F32)
     keep = I - GI
     order = [af[e * I:e * I + keep] for e in range(R)] + [af[e * I + keep:(e + 1) * I] for e in range(R)]
-    mats[3] = jnp.concatenate(order, axis=0).T.astype(BF16)
+    at_out[...] = jnp.concatenate(order, axis=0).T.astype(BF16)
     for e in (1, 2):
-        mats[3 + e] = mats[e].T
-    save_at = pltpu.make_async_copy(at, at_out, asem)
-    save_at.start()
+        mats[2 + e] = mats[e].T
 
     my_y = pl.ds(pl.multiple_of(me_r * Y, Y), Y)
 
     def to_h5(g):
         return h5.at[:, pl.ds(pl.multiple_of(me_r * keep + g * GI, GI), GI), :]
 
-    def own_copy(g, slot):
-        return pltpu.make_async_copy(tx4.at[slot, my_y], to_h5(g), lsem.at[slot])
-
-    def own_copy_b(q):
-        return pltpu.make_async_copy(
-            tx4b.at[q, :, my_y, :], h5b.at[pl.ds(me_r * GI + q * CI, CI)], lsem5.at[q])
-
     def free2(slot):
         wait_bytes(tx2.at[slot, :, pl.ds(0, J * (C - 1)), :], s2.at[slot])
 
@@ -159,7 +158,6 @@
 
     def free4(g, slot):
         wait_bytes(tx4.at[slot, pl.ds(0, Y * (R - 1))], s4.at[slot])
-        own_copy(g, slot).wait()
 
     per = GI // CI
 
@@ -171,14 +169,14 @@
         @pl.when(k < n)
         def _():
             slot = lax.rem(k, SLOTS)
-            rx1[k, :, my_y, :] = tx1[pl.ds(me_r * I + k * CI, CI), :, :]
-            wait_bytes(rx1.at[k, :, pl.ds(0, Y * (R - 1)), :], r1.at[k])
+            rx1[pl.ds(k * CI, CI), my_y, :] = tx1[pl.ds(me_r * I + k * CI, CI), :, :]
+            wait_bytes(rx1.at[pl.ds(0, CI), pl.ds(0, Y * (R - 1)), :], r1.at[k])
 
             @pl.when(k >= SLOTS)
             def _():
                 free2(slot)
 
-            res = dot(b[...], jnp.concatenate([rx1[k, i] for i in range(CI)], axis=1)).astype(BF16)
+            res = dot(b[...], jnp.concatenate([rx1[k * CI + i] for i in range(CI)], axis=1)).astype(BF16)
             for i in range(CI):
                 tx2[slot, i] = res[:, i * Z:(i + 1) * Z]
             for off in (2, 1, 3):
@@ -213,16 +211,16 @@
             for off in (2, 1, 3):
                 p = col_peer(off)
                 pltpu.make_async_remote_copy(
-                    src_ref=tx3.at[slot, p], dst_ref=rx3.at[m, :, pl.ds(pl.multiple_of(me_c * J, J), J), :],
+                    src_ref=tx3.at[slot, p], dst_ref=rx3.at[pl.ds(m * CI, CI), pl.ds(pl.multiple_of(me_c * J, J), J), :],
                     send_sem=s3.at[slot], recv_sem=r3.at[m], device_id={"col": p}, device_id_type=MESH).start()
-            rx3[m, :, pl.ds(pl.multiple_of(me_c * J, J), J), :] = tx3[slot, me_c]
+            rx3[pl.ds(m * CI, CI), pl.ds(pl.multiple_of(me_c * J, J), J), :] = tx3[slot, me_c]
 
         o = k - LAG5
 
         @pl.when(o >= 0)
         def _():
-            wait_bytes(rx3.at[o, :, pl.ds(0, J * (C - 1)), :], r3.at[o])
-            res = dot(bt[...], jnp.concatenate([rx3[o, i] for i in range(CI)], axis=1))
+            wait_bytes(rx3.at[pl.ds(0, CI), pl.ds(0, J * (C - 1)), :], r3.at[o])
+            res = dot(bt[...], jnp.concatenate([rx3[o * CI + i] for i in range(CI)], axis=1))
             g, q = lax.div(o, per), lax.rem(o, per)
             slot = lax.rem(g, 2)
 
@@ -249,7 +247,7 @@
                     pltpu.make_async_remote_copy(
                         src_ref=tx4.at[slot, pl.ds(pl.multiple_of(p * Y, Y), Y)], dst_ref=to_h5(g),
                         send_sem=s4.at[slot], recv_sem=r4, device_id={"row": p}, device_id_type=MESH).start()
-                own_copy(g, slot).start()
+                to_h5(g)[...] = tx4[slot, my_y]
 
             @pl.when(o >= n - per)
             def _():
@@ -261,17 +259,15 @@
                         src_ref=tx4b.at[q, :, pl.ds(pl.multiple_of(p * Y, Y), Y), :],
                         dst_ref=h5b.at[pl.ds(me_r * GI + q * CI, CI)],
                         send_sem=s5, recv_sem=r5, device_id={"row": p}, device_id_type=MESH).start()
-                own_copy_b(q).start()
-
-        @pl.when(k < Y // TY - 1)
-        def _():
-            second(k + 1)
+                h5b[pl.ds(me_r * GI + q * CI, CI)] = tx4b[q, :, my_y, :]
+
+        for t in range(1, Y // TY):
+            pl.when(k == t - 1)(functools.partial(second, t))
 
         return 0
 
     lax.fori_loop(0, n + LAG5, step, 0)
 
-    save_at.wait()
     wait_bytes(tx1.at[pl.ds(0, I * (R - 1))], s1)
     for m in range(n - SLOTS, n):
         free2(m % SLOTS)
@@ -279,8 +275,6 @@
     groups = I // GI - 1
     for g in (groups - 2, groups - 1):
         free4(g, g % 2)
-    for q in range(per):
-        own_copy_b(q).wait()
     wait_bytes(tx4b.at[:, :, pl.ds(0, Y * (R - 1)), :], s5)
     wait_bytes(h5.at[:, pl.ds(0, keep * (R - 1)), :], r4)
     wait_bytes(h5b.at[pl.ds(0, GI * (R - 1))], r5)
@@ -291,43 +285,43 @@
     I, J, N = d.shape
     n = I // CI
     hb = pl.BlockSpec(memory_space=pl.ANY)
+    vm = pl.BlockSpec(memory_space=pltpu.VMEM)
     DMA = pltpu.SemaphoreType.DMA
     return pl.pallas_call(
         functools.partial(exchange_kernel, R, C),
         name="exchange",
-        out_shape=(jax.ShapeDtypeStruct((Y, N - R * GI, Z), BF16), jax.ShapeDtypeStruct((R * GI, Y, Z), BF16),
-                   jax.ShapeDtypeStruct((X, N), BF16)),
+        out_shape=(pltpu.VMEM((Y, N - R * GI, Z), BF16), pltpu.VMEM((R * GI, Y, Z), BF16), pltpu.VMEM((X, N), BF16)),
         in_specs=[hb] * 5,
-        out_specs=(hb, hb, hb),
+        out_specs=(vm, vm, vm),
         scratch_shapes=[
-            pltpu.VMEM((6, N, X), BF16),
+            pltpu.VMEM((5, N, X), BF16),
             pltpu.VMEM((2, X, TY, Z), BF16),
-            pltpu.VMEM((Y // 8, X, 8 * Z), BF16),
-            pltpu.VMEM((TY // 8, X * 8, Z), F32),
-            pltpu.VMEM((TY // 8, N // 2 * 8, Z), F32),
+            pltpu.VMEM((TY // 8, X * PITCH, Z), F32),
+            pltpu.VMEM((TY // 8, N // 2 * PITCH, Z), F32),
             pltpu.VMEM((N, Y, Z), BF16),
-            pltpu.VMEM((n, CI, N, Z), BF16),
+            pltpu.VMEM((I, N, Z), BF16),
             pltpu.VMEM((SLOTS, CI, N, Z), BF16),
             pltpu.VMEM((n, C, CI, J, Z), BF16),
             pltpu.VMEM((SLOTS, C, CI, J, Z), BF16),
-            pltpu.VMEM((n, CI, N, Z), BF16),
+            pltpu.VMEM((I, N, Z), BF16),
             pltpu.VMEM((2, N, GI, Z), BF16),
             pltpu.VMEM((GI // CI, CI, N, Z), BF16),
             pltpu.VMEM((SLOTS, CI, J, N), F32),
             DMA((3,)), DMA((2,)), DMA((SLOTS,)), DMA, DMA((n,)), DMA((SLOTS,)), DMA((n,)), DMA((SLOTS,)), DMA((n,)),
-            DMA((2,)), DMA, DMA((2,)), DMA, DMA, DMA((GI // CI,)), DMA,
+            DMA((2,)), DMA, DMA, DMA,
         ],
         compiler_params=pltpu.CompilerParams(
-            collective_id=0, has_side_effects=True, vmem_limit_bytes=67043328),
+            collective_id=0, has_side_effects=True, vmem_limit_bytes=67043328 - 9 * 2**20),
     )(u, a, b, c, d)
 
 
-def last_kernel(at, h, hb, w, sc):
-    T, K, Z = h.shape
+def last_kernel(T, at, h, hb, w, sc):
+    K, Z = h.shape[1:]
     Kb, X = hb.shape[0], w.shape[0]
-    sc[...] = hb[...].astype(F32).reshape(Kb * T, Z)
+    y0 = pl.multiple_of(pl.program_id(0) * T, T)
+    sc[...] = hb[:, pl.ds(y0, T), :].astype(F32).reshape(Kb * T, Z)
     rhs = jnp.concatenate(
-        [jnp.concatenate([h[e], sc[pl.ds(e, Kb, stride=T), :].astype(BF16)], axis=0) for e in range(T)], axis=1)
+        [jnp.concatenate([h[y0 + e], sc[pl.ds(e, Kb, stride=T), :].astype(BF16)], axis=0) for e in range(T)], axis=1)
     res = dot(at[...], rhs)
     flat = w.reshape(X * T, Z)
     for e in range(T):
@@ -338,17 +332,18 @@
     Y, K, Z = h.shape
     Kb, X = hb.shape[0], at.shape[0]
     T = 8
+    vm = pl.BlockSpec(memory_space=pltpu.VMEM)
+    inputs = [pltpu.with_memory_space_constraint(v, pltpu.VMEM) for v in (at, h, hb)]
     return pl.pallas_call(
-        last_kernel,
+        functools.partial(last_kernel, T),
         name="last",
         grid=(Y // T,),
         out_shape=jax.ShapeDtypeStruct((X, Y, Z), F32),
-        in_specs=[pl.BlockSpec((X, K + Kb), lambda t: (0, 0)), pl.BlockSpec((T, K, Z), lambda t: (t, 0, 0)),
-                  pl.BlockSpec((Kb, T, Z), lambda t: (0, t, 0))],
+        in_specs=[vm, vm, vm],
         out_specs=pl.BlockSpec((X, T, Z), lambda t: (0, t, 0)),
         scratch_shapes=[pltpu.VMEM((Kb * T, Z), F32)],
-        compiler_params=pltpu.CompilerParams(vmem_limit_bytes=62 * 2**20),
-    )(at, h, hb)
+        compiler_params=pltpu.CompilerParams(vmem_limit_bytes=32 * 2**20),
+    )(*inputs)
 
 
 def solution(mesh):

time: 225 us -> 220 us (0.978)
  Pallas kernels: 225 us -> 220 us
    pallas_call x1, Pallas kernels: 13.1 us -> 9.39 us  [last(): pl.pallas_call(functools.partial(last_kernel, T), name='last', grid=(Y //...]
where the time goes in v4:
time: 220 us
  Pallas kernels  220 us (100%)
    pallas_call x1, Pallas kernels, exchange(): pl.pallas_call(functools.partial(exchange_kernel, R, C), name='exchange',...  210 us
    pallas_call x1, Pallas kernels, last(): pl.pallas_call(functools.partial(last_kernel, T), name='last', grid=(Y //...  9.39 us

profile of v4, /device:TPU:97, one launch (start us, length us, event | category | flops | bytes accessed | tf_op | source)
XLA Modules:
  0.0 219.5 jit_solution(9186177681785394119)
XLA Ops:
  0.0 210.1 %exchange.1 = (bf16[64,448,128]{2,1,0:T(8,128)(2,1)S(1)}, bf16[64,64,128]{2,1,0:T(8,128)(2,1)S(1)}, bf16[512,512]{1,0:T(8,128)(2,1)S(1)}) custom-call(bf16[512,64,128]{2,1,0:T(8,128)(2,1)} %bitcast.2, bf16[512,512]{1,0:T(8,128)(2,1)} %a_hbm.1, bf16[512,512]{1,0:T(8,128)(2,1)} %b_hbm.1, bf16[512,512]{1,0:T(8,128)(2,1)} %c_hbm.1, f32[64,128,512]{2,1,0:T(8,128)} %d.1), custom_call_target="tpu_custom_call" | custom-call | tf_op jit(solution)/shard_map/exchange/pallas_call | solution.py:290
  210.1 9.4 %last.1 = f32[512,64,128]{2,1,0:T(8,128)} custom-call(bf16[512,512]{1,0:T(8,128)(2,1)S(1)} %get-tuple-element.8.at, bf16[64,448,128]{2,1,0:T(8,128)(2,1)S(1)} %get-tuple-element.9.h, bf16[64,64,128]{2,1,0:T(8,128)(2,1)S(1)} %get-tuple-element.10.hb), custom_call_target="tpu_custom_call" | custom-call | tf_op jit(solution)/shard_map/last/pallas_call | solution.py:337

commit v5 on v4

--- a/solution.py
+++ b/solution.py
@@ -15,7 +15,7 @@
 GI = 8
 AHEAD = 4
 EARLY = 2
-LAG3, LAG5 = 1, 3
+DPRE = 3
 SLOTS = 4
 
 
@@ -132,7 +132,7 @@
 
     for k in range(EARLY, AHEAD):
         send_row(k, 0, Y)
-    for k in range(LAG3 + 2):
+    for k in range(DPRE):
         load_d(k).start()
 
     second(0)
@@ -186,15 +186,12 @@
                     send_sem=s2.at[slot], recv_sem=r2.at[k], device_id={"col": p}, device_id_type=MESH).start()
             rx2[k, me_c] = tx2[slot, :, pl.ds(pl.multiple_of(me_c * J, J), J), :]
 
-        m = k - LAG3
-
-        @pl.when(jnp.logical_and(m >= 0, m < n))
-        def _():
+        def middle(m, _):
             slot = lax.rem(m, SLOTS)
 
-            @pl.when(m + LAG3 + 2 < n)
-            def _():
-                load_d(m + LAG3 + 2).start()
+            @pl.when(m + DPRE < n)
+            def _():
+                load_d(m + DPRE).start()
 
             load_d(m).wait()
             wait_bytes(rx2.at[m, pl.ds(0, C - 1)], r2.at[m])
@@ -214,11 +211,14 @@
                     src_ref=tx3.at[slot, p], dst_ref=rx3.at[pl.ds(m * CI, CI), pl.ds(pl.multiple_of(me_c * J, J), J), :],
                     send_sem=s3.at[slot], recv_sem=r3.at[m], device_id={"col": p}, device_id_type=MESH).start()
             rx3[pl.ds(m * CI, CI), pl.ds(pl.multiple_of(me_c * J, J), J), :] = tx3[slot, me_c]
-
-        o = k - LAG5
-
-        @pl.when(o >= 0)
-        def _():
+            return 0
+
+        turn = n // 2
+        lo = jnp.maximum(jnp.where(k <= turn, k - 2, k - 1), 0)
+        hi = jnp.minimum(jnp.where(k < turn, k - 1, k), n)
+        lax.fori_loop(lo, hi, middle, 0)
+
+        def late(o, _):
             wait_bytes(rx3.at[pl.ds(0, CI), pl.ds(0, J * (C - 1)), :], r3.at[o])
             res = dot(bt[...], jnp.concatenate([rx3[o * CI + i] for i in range(CI)], axis=1))
             g, q = lax.div(o, per), lax.rem(o, per)
@@ -260,13 +260,18 @@
                         dst_ref=h5b.at[pl.ds(me_r * GI + q * CI, CI)],
                         send_sem=s5, recv_sem=r5, device_id={"row": p}, device_id_type=MESH).start()
                 h5b[pl.ds(me_r * GI + q * CI, CI)] = tx4b[q, :, my_y, :]
+            return 0
+
+        lo5 = jnp.maximum(jnp.where(k <= turn + 1, k - 3, k - 2), 0)
+        hi5 = jnp.minimum(jnp.where(k < turn + 1, k - 2, k - 1), n)
+        lax.fori_loop(lo5, hi5, late, 0)
 
         for t in range(1, Y // TY):
             pl.when(k == t - 1)(functools.partial(second, t))
 
         return 0
 
-    lax.fori_loop(0, n + LAG5, step, 0)
+    lax.fori_loop(0, n + 2, step, 0)
 
     wait_bytes(tx1.at[pl.ds(0, I * (R - 1))], s1)
     for m in range(n - SLOTS, n):

time: 220 us -> 216 us (0.982)
  Pallas kernels: 220 us -> 216 us
    pallas_call x1, Pallas kernels: 210 us -> 207 us  [exchange(): pl.pallas_call(functools.partial(exchange_kernel, R, C), name='exchange',...]
where the time goes in v5:
time: 216 us
  Pallas kernels  216 us (100%)
    pallas_call x1, Pallas kernels, exchange(): pl.pallas_call(functools.partial(exchange_kernel, R, C), name='exchange',...  207 us
    pallas_call x1, Pallas kernels, last(): pl.pallas_call(functools.partial(last_kernel, T), name='last', grid=(Y //...  9.37 us

profile of v5, /device:TPU:97, one launch (start us, length us, event | category | flops | bytes accessed | tf_op | source)
XLA Modules:
  0.0 216.3 jit_solution(10762194374234448411)
XLA Ops:
  0.0 206.9 %exchange.1 = (bf16[64,448,128]{2,1,0:T(8,128)(2,1)S(1)}, bf16[64,64,128]{2,1,0:T(8,128)(2,1)S(1)}, bf16[512,512]{1,0:T(8,128)(2,1)S(1)}) custom-call(bf16[512,64,128]{2,1,0:T(8,128)(2,1)} %bitcast.2, bf16[512,512]{1,0:T(8,128)(2,1)} %a_hbm.1, bf16[512,512]{1,0:T(8,128)(2,1)} %b_hbm.1, bf16[512,512]{1,0:T(8,128)(2,1)} %c_hbm.1, f32[64,128,512]{2,1,0:T(8,128)} %d.1), custom_call_target="tpu_custom_call" | custom-call | tf_op jit(solution)/shard_map/exchange/pallas_call | solution.py:295
  206.9 9.4 %last.1 = f32[512,64,128]{2,1,0:T(8,128)} custom-call(bf16[512,512]{1,0:T(8,128)(2,1)S(1)} %get-tuple-element.8.at, bf16[64,448,128]{2,1,0:T(8,128)(2,1)S(1)} %get-tuple-element.9.h, bf16[64,64,128]{2,1,0:T(8,128)(2,1)S(1)} %get-tuple-element.10.hb), custom_call_target="tpu_custom_call" | custom-call | tf_op jit(solution)/shard_map/last/pallas_call | solution.py:342

commit v6 on v5

--- a/solution.py
+++ b/solution.py
@@ -14,8 +14,11 @@
 PITCH = 9
 GI = 8
 AHEAD = 4
-EARLY = 2
+EARLY = 1
 DPRE = 3
+LAG0, LAG1, LAG5 = 2, 1, 1
+XPARTS = 2
+BUFS = 3
 SLOTS = 4
 
 
@@ -205,27 +208,32 @@
             h4 = dot(h3, c[...]).astype(BF16)
             for e in range(C):
                 tx3[slot, e] = h4[:, e * Z:(e + 1) * Z].reshape(CI, J, Z)
-            for off in (2, 1, 3):
-                p = col_peer(off)
-                pltpu.make_async_remote_copy(
-                    src_ref=tx3.at[slot, p], dst_ref=rx3.at[pl.ds(m * CI, CI), pl.ds(pl.multiple_of(me_c * J, J), J), :],
-                    send_sem=s3.at[slot], recv_sem=r3.at[m], device_id={"col": p}, device_id_type=MESH).start()
+            for i in range(CI):
+                for off in (2, 1, 3):
+                    p = col_peer(off)
+                    pltpu.make_async_remote_copy(
+                        src_ref=tx3.at[slot, p, i], dst_ref=rx3.at[m * CI + i, pl.ds(pl.multiple_of(me_c * J, J), J), :],
+                        send_sem=s3.at[slot], recv_sem=r3.at[m * CI + i], device_id={"col": p}, device_id_type=MESH).start()
             rx3[pl.ds(m * CI, CI), pl.ds(pl.multiple_of(me_c * J, J), J), :] = tx3[slot, me_c]
             return 0
 
         turn = n // 2
-        lo = jnp.maximum(jnp.where(k <= turn, k - 2, k - 1), 0)
-        hi = jnp.minimum(jnp.where(k < turn, k - 1, k), n)
+        lo = jnp.maximum(jnp.where(k <= turn, k - LAG0, k - LAG1), 0)
+        hi = jnp.minimum(jnp.where(k < turn, k - LAG0, k - LAG1) + 1, n)
         lax.fori_loop(lo, hi, middle, 0)
 
         def late(o, _):
-            wait_bytes(rx3.at[pl.ds(0, CI), pl.ds(0, J * (C - 1)), :], r3.at[o])
-            res = dot(bt[...], jnp.concatenate([rx3[o * CI + i] for i in range(CI)], axis=1))
             g, q = lax.div(o, per), lax.rem(o, per)
             slot = lax.rem(g, 2)
 
+            def arrived(i):
+                wait_bytes(rx3.at[0, pl.ds(0, J * (C - 1)), :], r3.at[o * CI + i])
+
             @pl.when(o < n - per)
             def _():
+                for i in range(CI):
+                    arrived(i)
+                res = dot(bt[...], jnp.concatenate([rx3[o * CI + i] for i in range(CI)], axis=1))
                 for i in range(CI):
                     sa[0, pl.ds(q * CI + i, N, stride=GI), :] = res[:, i * Z:(i + 1) * Z]
 
@@ -252,18 +260,19 @@
             @pl.when(o >= n - per)
             def _():
                 for i in range(CI):
-                    tx4b[q, i] = res[:, i * Z:(i + 1) * Z].astype(BF16)
-                for off in (4, 5, 3, 2, 6, 7, 1):
-                    p = row_peer(off)
-                    pltpu.make_async_remote_copy(
-                        src_ref=tx4b.at[q, :, pl.ds(pl.multiple_of(p * Y, Y), Y), :],
-                        dst_ref=h5b.at[pl.ds(me_r * GI + q * CI, CI)],
-                        send_sem=s5, recv_sem=r5, device_id={"row": p}, device_id_type=MESH).start()
-                h5b[pl.ds(me_r * GI + q * CI, CI)] = tx4b[q, :, my_y, :]
-            return 0
-
-        lo5 = jnp.maximum(jnp.where(k <= turn + 1, k - 3, k - 2), 0)
-        hi5 = jnp.minimum(jnp.where(k < turn + 1, k - 2, k - 1), n)
+                    arrived(i)
+                    tx4b[q, i] = dot(bt[...], rx3[o * CI + i]).astype(BF16)
+                    row = me_r * GI + q * CI + i
+                    for off in (4, 5, 3, 2, 6, 7, 1):
+                        p = row_peer(off)
+                        pltpu.make_async_remote_copy(
+                            src_ref=tx4b.at[q, i, pl.ds(pl.multiple_of(p * Y, Y), Y), :], dst_ref=h5b.at[row],
+                            send_sem=s5, recv_sem=r5, device_id={"row": p}, device_id_type=MESH).start()
+                    h5b[row] = tx4b[q, i, my_y, :]
+            return 0
+
+        lo5 = jnp.maximum(jnp.where(k <= turn, k - LAG0, k - LAG1) - LAG5, 0)
+        hi5 = jnp.minimum(jnp.where(k < turn, k - LAG0, k - LAG1) - LAG5 + 1, n)
         lax.fori_loop(lo5, hi5, late, 0)
 
         for t in range(1, Y // TY):
@@ -271,7 +280,7 @@
 
         return 0
 
-    lax.fori_loop(0, n + 2, step, 0)
+    lax.fori_loop(0, n + LAG1 + LAG5, step, 0)
 
     wait_bytes(tx1.at[pl.ds(0, I * (R - 1))], s1)
     for m in range(n - SLOTS, n):
@@ -312,7 +321,7 @@
             pltpu.VMEM((2, N, GI, Z), BF16),
             pltpu.VMEM((GI // CI, CI, N, Z), BF16),
             pltpu.VMEM((SLOTS, CI, J, N), F32),
-            DMA((3,)), DMA((2,)), DMA((SLOTS,)), DMA, DMA((n,)), DMA((SLOTS,)), DMA((n,)), DMA((SLOTS,)), DMA((n,)),
+            DMA((3,)), DMA((2,)), DMA((SLOTS,)), DMA, DMA((n,)), DMA((SLOTS,)), DMA((n,)), DMA((SLOTS,)), DMA((I,)),
             DMA((2,)), DMA, DMA, DMA,
         ],
         compiler_params=pltpu.CompilerParams(
@@ -320,17 +329,33 @@
     )(u, a, b, c, d)
 
 
-def last_kernel(T, at, h, hb, w, sc):
-    K, Z = h.shape[1:]
+def last_kernel(at, h, hb, w, buf, sc, sem):
+    Y, K, Z = h.shape
     Kb, X = hb.shape[0], w.shape[0]
-    y0 = pl.multiple_of(pl.program_id(0) * T, T)
-    sc[...] = hb[:, pl.ds(y0, T), :].astype(F32).reshape(Kb * T, Z)
-    rhs = jnp.concatenate(
-        [jnp.concatenate([h[y0 + e], sc[pl.ds(e, Kb, stride=T), :].astype(BF16)], axis=0) for e in range(T)], axis=1)
-    res = dot(at[...], rhs)
-    flat = w.reshape(X * T, Z)
-    for e in range(T):
-        flat[pl.ds(e, X, stride=T), :] = res[:, e * Z:(e + 1) * Z]
+    XB = X // XPARTS
+    T = buf.shape[2]
+    copies = []
+    for t in range(Y // T):
+        slot = t % BUFS
+        if t >= BUFS:
+            for copy in copies[t - BUFS]:
+                copy.wait()
+        sc[...] = hb[:, t * T:(t + 1) * T, :].astype(F32).reshape(Kb * T, Z)
+        rhs = jnp.concatenate(
+            [jnp.concatenate([h[t * T + e], sc[pl.ds(e, Kb, stride=T), :].astype(BF16)], axis=0) for e in range(T)], axis=1)
+        flat = buf.at[slot].reshape(X * T, Z)
+        copies.append([])
+        for m in range(XPARTS):
+            res = dot(at[m * XB:(m + 1) * XB, :], rhs)
+            for e in range(T):
+                flat[pl.ds(m * XB * T + e, XB, stride=T), :] = res[:, e * Z:(e + 1) * Z]
+            copy = pltpu.make_async_copy(
+                buf.at[slot, pl.ds(m * XB, XB)], w.at[pl.ds(m * XB, XB), pl.ds(t * T, T), :], sem.at[slot, m])
+            copy.start()
+            copies[t].append(copy)
+    for t in range(Y // T - BUFS, Y // T):
+        for copy in copies[t]:
+            copy.wait()
 
 
 def last(at, h, hb):
@@ -340,14 +365,14 @@
     vm = pl.BlockSpec(memory_space=pltpu.VMEM)
     inputs = [pltpu.with_memory_space_constraint(v, pltpu.VMEM) for v in (at, h, hb)]
     return pl.pallas_call(
-        functools.partial(last_kernel, T),
+        last_kernel,
         name="last",
-        grid=(Y // T,),
         out_shape=jax.ShapeDtypeStruct((X, Y, Z), F32),
         in_specs=[vm, vm, vm],
-        out_specs=pl.BlockSpec((X, T, Z), lambda t: (0, t, 0)),
-        scratch_shapes=[pltpu.VMEM((Kb * T, Z), F32)],
-        compiler_params=pltpu.CompilerParams(vmem_limit_bytes=32 * 2**20),
+        out_specs=pl.BlockSpec(memory_space=pl.ANY),
+        scratch_shapes=[pltpu.VMEM((BUFS, X, T, Z), F32), pltpu.VMEM((Kb * T, Z), F32),
+                        pltpu.SemaphoreType.DMA((BUFS, XPARTS))],
+        compiler_params=pltpu.CompilerParams(vmem_limit_bytes=40 * 2**20),
     )(*inputs)
 
 

time: 216 us -> 213 us (0.986)
  Pallas kernels: 216 us -> 213 us
    pallas_call x1, Pallas kernels: 9.37 us -> 6.94 us  [last(): pl.pallas_call(last_kernel, name='last', out_shape=jax.ShapeDtypeStruct((...]
where the time goes in v6:
time: 213 us
  Pallas kernels  213 us (100%)
    pallas_call x1, Pallas kernels, exchange(): pl.pallas_call(functools.partial(exchange_kernel, R, C), name='exchange',...  206 us
    pallas_call x1, Pallas kernels, last(): pl.pallas_call(last_kernel, name='last', out_shape=jax.ShapeDtypeStruct((...  6.94 us

profile of v6, /device:TPU:97, one launch (start us, length us, event | category | flops | bytes accessed | tf_op | source)
XLA Modules:
  0.0 212.7 jit_solution(7281709113115858400)
XLA Ops:
  0.0 205.7 %exchange.1 = (bf16[64,448,128]{2,1,0:T(8,128)(2,1)S(1)}, bf16[64,64,128]{2,1,0:T(8,128)(2,1)S(1)}, bf16[512,512]{1,0:T(8,128)(2,1)S(1)}) custom-call(bf16[512,64,128]{2,1,0:T(8,128)(2,1)} %bitcast.2, bf16[512,512]{1,0:T(8,128)(2,1)} %a_hbm.1, bf16[512,512]{1,0:T(8,128)(2,1)} %b_hbm.1, bf16[512,512]{1,0:T(8,128)(2,1)} %c_hbm.1, f32[64,128,512]{2,1,0:T(8,128)} %d.1), custom_call_target="tpu_custom_call" | custom-call | tf_op jit(solution)/shard_map/exchange/pallas_call | solution.py:304
  205.8 6.9 %last.1 = f32[512,64,128]{2,1,0:T(8,128)} custom-call(bf16[512,512]{1,0:T(8,128)(2,1)S(1)} %get-tuple-element.8.at, bf16[64,448,128]{2,1,0:T(8,128)(2,1)S(1)} %get-tuple-element.9.h, bf16[64,64,128]{2,1,0:T(8,128)(2,1)S(1)} %get-tuple-element.10.hb), custom_call_target="tpu_custom_call" | custom-call | tf_op jit(solution)/shard_map/last/pallas_call | solution.py:367

commit v7 on v6

--- a/solution.py
+++ b/solution.py
@@ -20,6 +20,8 @@
 XPARTS = 2
 BUFS = 3
 SLOTS = 4
+RING1, RING = 16, 8
+PARTS = 4
 
 
 def dot(a, b):
@@ -51,7 +53,10 @@
         slot = lax.rem(k, SLOTS)
         return pltpu.make_async_copy(d.at[pl.ds(k * CI, CI)], dbuf.at[slot], dsem.at[slot])
 
-    load_u(0).start()
+    first = [pltpu.make_async_copy(u.at[pl.ds(e * (X // 2), X // 2), pl.ds(0, TY), :],
+                                   ubuf.at[0, pl.ds(e * (X // 2), X // 2)], usem.at[2 * e]) for e in range(2)]
+    for copy in first:
+        copy.start()
     loads = [pltpu.make_async_copy(h, mats.at[e], msem.at[e]) for e, h in enumerate((a_hbm, b_hbm, c_hbm))]
     loads[0].start()
     load_u(1).start()
@@ -70,21 +75,21 @@
             pltpu.make_async_remote_copy(
                 src_ref=tx1.at[pl.ds(p * I + k * CI, CI), pl.ds(y0, ny), :],
                 dst_ref=rx1.at[pl.ds(k * CI, CI), pl.ds(pl.multiple_of(me_r * Y + y0, TY), ny), :],
-                send_sem=s1, recv_sem=r1.at[k], device_id={"row": p}, device_id_type=MESH).start()
-
-    H = I // 2
-
-    def project(half, h, rhs):
-        res = dot(jnp.concatenate([a[pl.ds(e * I + half * H, H), :] for e in range(R)], axis=0), rhs)
+                send_sem=s1, recv_sem=r1.at[lax.rem(k, RING1)], device_id={"row": p}, device_id_type=MESH).start()
+
+    H = I // PARTS
+
+    def project(part, h, rhs):
+        res = dot(jnp.concatenate([a[pl.ds(e * I + part * H, H), :] for e in range(R)], axis=0), rhs)
         for e in range(8):
             sb[h, pl.ds(e, R * H, stride=PITCH), :] = res[:, e * Z:(e + 1) * Z]
 
-    def gather(half, t):
+    def gather(part, t):
         def body(e, _):
             for i in range(H):
                 row = (e * H + i) * PITCH
                 parts = [sb[h, pl.ds(row, 8), :] for h in range(TY // 8)]
-                tx1[e * I + half * H + i, pl.ds(t * TY, TY), :] = jnp.concatenate(parts, axis=0).astype(BF16)
+                tx1[e * I + part * H + i, pl.ds(t * TY, TY), :] = jnp.concatenate(parts, axis=0).astype(BF16)
             return 0
 
         lax.fori_loop(0, R, body, 0)
@@ -93,16 +98,15 @@
         ref = rx3 if t < Y // TY // 2 else rx1
         return ref.at[I // 2 + (t % (Y // TY // 2)) * TY + h * 8 + e]
 
-    def second(t):
+    def second(part, t):
         def body(h, _):
-            project(1, h, jnp.concatenate([kept(t, h, e)[...] for e in range(8)], axis=1))
+            project(part, h, jnp.concatenate([kept(t, h, e)[...] for e in range(8)], axis=1))
             return 0
 
         lax.fori_loop(0, TY // 8, body, 0)
-        gather(1, t)
+        gather(part, t)
 
     for t in range(Y // TY):
-        load_u(t).wait()
         slot = t % 2
 
         def spread(g, _):
@@ -113,7 +117,14 @@
                     sa[h, pl.ds((x0 + x) * PITCH, 8), :] = v[x, h * 8:(h + 1) * 8, :]
             return 0
 
-        lax.fori_loop(0, X // 32, spread, 0)
+        if t == 0:
+            first[0].wait()
+            lax.fori_loop(0, X // 64, spread, 0)
+            first[1].wait()
+            lax.fori_loop(X // 64, X // 32, spread, 0)
+        else:
+            load_u(t).wait()
+            lax.fori_loop(0, X // 32, spread, 0)
         if t + 2 < Y // TY:
             load_u(t + 2).start()
         if t == 0:
@@ -126,7 +137,7 @@
             project(0, h, jnp.concatenate(cols, axis=1))
             return 0
 
-        lax.fori_loop(0, TY // 8, tile, 0)
+        lax.fori_loop(0, TY // 8, tile, 0, unroll=True)
         gather(0, t)
         if t == 0:
             pl.semaphore_wait(barrier, R - 1 + C - 1)
@@ -138,7 +149,9 @@
     for k in range(DPRE):
         load_d(k).start()
 
-    second(0)
+    rest = [(part, t) for part in range(1, PARTS) for t in range(Y // TY)]
+    for part, t in rest[:2]:
+        second(part, t)
     loads[1].wait()
     loads[2].wait()
     af = a[...].astype(F32)
@@ -173,7 +186,7 @@
         def _():
             slot = lax.rem(k, SLOTS)
             rx1[pl.ds(k * CI, CI), my_y, :] = tx1[pl.ds(me_r * I + k * CI, CI), :, :]
-            wait_bytes(rx1.at[pl.ds(0, CI), pl.ds(0, Y * (R - 1)), :], r1.at[k])
+            wait_bytes(rx1.at[pl.ds(0, CI), pl.ds(0, Y * (R - 1)), :], r1.at[lax.rem(k, RING1)])
 
             @pl.when(k >= SLOTS)
             def _():
@@ -186,7 +199,7 @@
                 p = col_peer(off)
                 pltpu.make_async_remote_copy(
                     src_ref=tx2.at[slot, :, pl.ds(pl.multiple_of(p * J, J), J), :], dst_ref=rx2.at[k, me_c],
-                    send_sem=s2.at[slot], recv_sem=r2.at[k], device_id={"col": p}, device_id_type=MESH).start()
+                    send_sem=s2.at[slot], recv_sem=r2.at[lax.rem(k, RING)], device_id={"col": p}, device_id_type=MESH).start()
             rx2[k, me_c] = tx2[slot, :, pl.ds(pl.multiple_of(me_c * J, J), J), :]
 
         def middle(m, _):
@@ -197,7 +210,7 @@
                 load_d(m + DPRE).start()
 
             load_d(m).wait()
-            wait_bytes(rx2.at[m, pl.ds(0, C - 1)], r2.at[m])
+            wait_bytes(rx2.at[m, pl.ds(0, C - 1)], r2.at[lax.rem(m, RING)])
 
             @pl.when(m >= SLOTS)
             def _():
@@ -213,7 +226,7 @@
                     p = col_peer(off)
                     pltpu.make_async_remote_copy(
                         src_ref=tx3.at[slot, p, i], dst_ref=rx3.at[m * CI + i, pl.ds(pl.multiple_of(me_c * J, J), J), :],
-                        send_sem=s3.at[slot], recv_sem=r3.at[m * CI + i], device_id={"col": p}, device_id_type=MESH).start()
+                        send_sem=s3.at[slot], recv_sem=r3.at[lax.rem(m, RING) * CI + i], device_id={"col": p}, device_id_type=MESH).start()
             rx3[pl.ds(m * CI, CI), pl.ds(pl.multiple_of(me_c * J, J), J), :] = tx3[slot, me_c]
             return 0
 
@@ -227,7 +240,7 @@
             slot = lax.rem(g, 2)
 
             def arrived(i):
-                wait_bytes(rx3.at[0, pl.ds(0, J * (C - 1)), :], r3.at[o * CI + i])
+                wait_bytes(rx3.at[0, pl.ds(0, J * (C - 1)), :], r3.at[lax.rem(o, RING) * CI + i])
 
             @pl.when(o < n - per)
             def _():
@@ -275,8 +288,8 @@
         hi5 = jnp.minimum(jnp.where(k < turn, k - LAG0, k - LAG1) - LAG5 + 1, n)
         lax.fori_loop(lo5, hi5, late, 0)
 
-        for t in range(1, Y // TY):
-            pl.when(k == t - 1)(functools.partial(second, t))
+        for e in range(2, len(rest)):
+            pl.when(k == (e - 2) // 2)(functools.partial(second, *rest[e]))
 
         return 0
 
@@ -311,7 +324,7 @@
             pltpu.VMEM((5, N, X), BF16),
             pltpu.VMEM((2, X, TY, Z), BF16),
             pltpu.VMEM((TY // 8, X * PITCH, Z), F32),
-            pltpu.VMEM((TY // 8, N // 2 * PITCH, Z), F32),
+            pltpu.VMEM((TY // 8, N // PARTS * PITCH, Z), F32),
             pltpu.VMEM((N, Y, Z), BF16),
             pltpu.VMEM((I, N, Z), BF16),
             pltpu.VMEM((SLOTS, CI, N, Z), BF16),
@@ -321,7 +334,8 @@
             pltpu.VMEM((2, N, GI, Z), BF16),
             pltpu.VMEM((GI // CI, CI, N, Z), BF16),
             pltpu.VMEM((SLOTS, CI, J, N), F32),
-            DMA((3,)), DMA((2,)), DMA((SLOTS,)), DMA, DMA((n,)), DMA((SLOTS,)), DMA((n,)), DMA((SLOTS,)), DMA((I,)),
+            DMA((3,)), DMA((3,)), DMA((SLOTS,)), DMA, DMA((RING1,)), DMA((SLOTS,)), DMA((RING,)), DMA((SLOTS,)),
+            DMA((RING * CI,)),
             DMA((2,)), DMA, DMA, DMA,
         ],
         compiler_params=pltpu.CompilerParams(

time: 213 us -> 210 us (0.986)
  Pallas kernels: 213 us -> 210 us
    pallas_call x1, Pallas kernels: 206 us -> 203 us  [exchange(): pl.pallas_call(functools.partial(exchange_kernel, R, C), name='exchange',...]
where the time goes in v7:
time: 210 us
  Pallas kernels  210 us (100%)
    pallas_call x1, Pallas kernels, exchange(): pl.pallas_call(functools.partial(exchange_kernel, R, C), name='exchange',...  203 us
    pallas_call x1, Pallas kernels, last(): pl.pallas_call(last_kernel, name='last', out_shape=jax.ShapeDtypeStruct((...  6.92 us

profile of v7, /device:TPU:97, one launch (start us, length us, event | category | flops | bytes accessed | tf_op | source)
XLA Modules:
  0.0 210.3 jit_solution(15621266290139469405)
XLA Ops:
  0.0 203.2 %exchange.1 = (bf16[64,448,128]{2,1,0:T(8,128)(2,1)S(1)}, bf16[64,64,128]{2,1,0:T(8,128)(2,1)S(1)}, bf16[512,512]{1,0:T(8,128)(2,1)S(1)}) custom-call(bf16[512,64,128]{2,1,0:T(8,128)(2,1)} %bitcast.2, bf16[512,512]{1,0:T(8,128)(2,1)} %a_hbm.1, bf16[512,512]{1,0:T(8,128)(2,1)} %b_hbm.1, bf16[512,512]{1,0:T(8,128)(2,1)} %c_hbm.1, f32[64,128,512]{2,1,0:T(8,128)} %d.1), custom_call_target="tpu_custom_call" | custom-call | tf_op jit(solution)/shard_map/exchange/pallas_call | solution.py:317
  203.2 6.9 %last.1 = f32[512,64,128]{2,1,0:T(8,128)} custom-call(bf16[512,512]{1,0:T(8,128)(2,1)S(1)} %get-tuple-element.8.at, bf16[64,448,128]{2,1,0:T(8,128)(2,1)S(1)} %get-tuple-element.9.h, bf16[64,64,128]{2,1,0:T(8,128)(2,1)S(1)} %get-tuple-element.10.hb), custom_call_target="tpu_custom_call" | custom-call | tf_op jit(solution)/shard_map/last/pallas_call | solution.py:381

commit v8 on v7

--- a/solution.py
+++ b/solution.py
@@ -18,7 +18,7 @@
 DPRE = 3
 LAG0, LAG1, LAG5 = 2, 1, 1
 XPARTS = 2
-BUFS = 3
+BUFS = 4
 SLOTS = 4
 RING1, RING = 16, 8
 PARTS = 4
@@ -28,12 +28,16 @@
     return jnp.dot(a, b, preferred_element_type=F32)
 
 
+def far_first(n):
+    return sorted(range(1, n), key=lambda off: -min(off, n - off))
+
+
 def wait_bytes(ref, sem):
     pltpu.make_async_copy(ref, ref, sem).wait()
 
 
 def exchange_kernel(R, C, u, a_hbm, b_hbm, c_hbm, d, h5, h5b, at_out, mats, ubuf, sa, sb, tx1, rx1, tx2, rx2, tx3, rx3,
-                    tx4, tx4b, dbuf, msem, usem, dsem, s1, r1, s2, r2, s3, r3, s4, r4, s5, r5):
+                    tx4, tx4b, dbuf, msem, fsem, usem, dsem, s1, r1, s2, r2, s3, r3, s4, r4, s5, r5):
     X, Y, Z = u.shape
     I, J, N = d.shape
     n = I // CI
@@ -53,8 +57,9 @@
         slot = lax.rem(k, SLOTS)
         return pltpu.make_async_copy(d.at[pl.ds(k * CI, CI)], dbuf.at[slot], dsem.at[slot])
 
-    first = [pltpu.make_async_copy(u.at[pl.ds(e * (X // 2), X // 2), pl.ds(0, TY), :],
-                                   ubuf.at[0, pl.ds(e * (X // 2), X // 2)], usem.at[2 * e]) for e in range(2)]
+    XQ = X // 4
+    first = [pltpu.make_async_copy(u.at[pl.ds(e * XQ, XQ), pl.ds(0, TY), :],
+                                   ubuf.at[0, pl.ds(e * XQ, XQ)], fsem.at[e]) for e in range(4)]
     for copy in first:
         copy.start()
     loads = [pltpu.make_async_copy(h, mats.at[e], msem.at[e]) for e, h in enumerate((a_hbm, b_hbm, c_hbm))]
@@ -118,13 +123,12 @@
             return 0
 
         if t == 0:
-            first[0].wait()
-            lax.fori_loop(0, X // 64, spread, 0)
-            first[1].wait()
-            lax.fori_loop(X // 64, X // 32, spread, 0)
+            for e in range(4):
+                first[e].wait()
+                lax.fori_loop(e * XQ // 32, (e + 1) * XQ // 32, spread, 0, unroll=True)
         else:
             load_u(t).wait()
-            lax.fori_loop(0, X // 32, spread, 0)
+            lax.fori_loop(0, X // 32, spread, 0, unroll=4)
         if t + 2 < Y // TY:
             load_u(t + 2).start()
         if t == 0:
@@ -139,10 +143,13 @@
 
         lax.fori_loop(0, TY // 8, tile, 0, unroll=True)
         gather(0, t)
-        if t == 0:
+        if t == 1:
             pl.semaphore_wait(barrier, R - 1 + C - 1)
         for k in range(EARLY):
-            send_row(k, t * TY, TY)
+            if t == 1:
+                send_row(k, 0, 2 * TY)
+            elif t > 1:
+                send_row(k, t * TY, TY)
 
     for k in range(EARLY, AHEAD):
         send_row(k, 0, Y)
@@ -195,7 +202,7 @@
             res = dot(b[...], jnp.concatenate([rx1[k * CI + i] for i in range(CI)], axis=1)).astype(BF16)
             for i in range(CI):
                 tx2[slot, i] = res[:, i * Z:(i + 1) * Z]
-            for off in (2, 1, 3):
+            for off in far_first(C):
                 p = col_peer(off)
                 pltpu.make_async_remote_copy(
                     src_ref=tx2.at[slot, :, pl.ds(pl.multiple_of(p * J, J), J), :], dst_ref=rx2.at[k, me_c],
@@ -222,7 +229,7 @@
             for e in range(C):
                 tx3[slot, e] = h4[:, e * Z:(e + 1) * Z].reshape(CI, J, Z)
             for i in range(CI):
-                for off in (2, 1, 3):
+                for off in far_first(C):
                     p = col_peer(off)
                     pltpu.make_async_remote_copy(
                         src_ref=tx3.at[slot, p, i], dst_ref=rx3.at[m * CI + i, pl.ds(pl.multiple_of(me_c * J, J), J), :],
@@ -263,7 +270,7 @@
                     return 0
 
                 lax.fori_loop(0, N // 32, pack, 0)
-                for off in (4, 5, 3, 2, 6, 7, 1):
+                for off in far_first(R):
                     p = row_peer(off)
                     pltpu.make_async_remote_copy(
                         src_ref=tx4.at[slot, pl.ds(pl.multiple_of(p * Y, Y), Y)], dst_ref=to_h5(g),
@@ -276,7 +283,7 @@
                     arrived(i)
                     tx4b[q, i] = dot(bt[...], rx3[o * CI + i]).astype(BF16)
                     row = me_r * GI + q * CI + i
-                    for off in (4, 5, 3, 2, 6, 7, 1):
+                    for off in far_first(R):
                         p = row_peer(off)
                         pltpu.make_async_remote_copy(
                             src_ref=tx4b.at[q, i, pl.ds(pl.multiple_of(p * Y, Y), Y), :], dst_ref=h5b.at[row],
@@ -334,7 +341,7 @@
             pltpu.VMEM((2, N, GI, Z), BF16),
             pltpu.VMEM((GI // CI, CI, N, Z), BF16),
             pltpu.VMEM((SLOTS, CI, J, N), F32),
-            DMA((3,)), DMA((3,)), DMA((SLOTS,)), DMA, DMA((RING1,)), DMA((SLOTS,)), DMA((RING,)), DMA((SLOTS,)),
+            DMA((3,)), DMA((4,)), DMA((2,)), DMA((SLOTS,)), DMA, DMA((RING1,)), DMA((SLOTS,)), DMA((RING,)), DMA((SLOTS,)),
             DMA((RING * CI,)),
             DMA((2,)), DMA, DMA, DMA,
         ],

time: 210 us -> 210 us (level)
  no operation moved by 1% of the time
where the time goes in v8:
time: 210 us
  Pallas kernels  210 us (100%)
    pallas_call x1, Pallas kernels, exchange(): pl.pallas_call(functools.partial(exchange_kernel, R, C), name='exchange',...  203 us
    pallas_call x1, Pallas kernels, last(): pl.pallas_call(last_kernel, name='last', out_shape=jax.ShapeDtypeStruct((...  6.83 us

profile of v8, /device:TPU:97, one launch (start us, length us, event | category | flops | bytes accessed | tf_op | source)
XLA Modules:
  0.0 210.0 jit_solution(1780093736709641748)
XLA Ops:
  0.0 203.0 %exchange.1 = (bf16[64,448,128]{2,1,0:T(8,128)(2,1)S(1)}, bf16[64,64,128]{2,1,0:T(8,128)(2,1)S(1)}, bf16[512,512]{1,0:T(8,128)(2,1)S(1)}) custom-call(bf16[512,64,128]{2,1,0:T(8,128)(2,1)} %bitcast.2, bf16[512,512]{1,0:T(8,128)(2,1)} %a_hbm.1, bf16[512,512]{1,0:T(8,128)(2,1)} %b_hbm.1, bf16[512,512]{1,0:T(8,128)(2,1)} %c_hbm.1, f32[64,128,512]{2,1,0:T(8,128)} %d.1), custom_call_target="tpu_custom_call" | custom-call | tf_op jit(solution)/shard_map/exchange/pallas_call | solution.py:324
  203.0 6.8 %last.1 = f32[512,64,128]{2,1,0:T(8,128)} custom-call(bf16[512,512]{1,0:T(8,128)(2,1)S(1)} %get-tuple-element.8.at, bf16[64,448,128]{2,1,0:T(8,128)(2,1)S(1)} %get-tuple-element.9.h, bf16[64,64,128]{2,1,0:T(8,128)(2,1)S(1)} %get-tuple-element.10.hb), custom_call_target="tpu_custom_call" | custom-call | tf_op jit(solution)/shard_map/last/pallas_call | solution.py:388

commit v9 on v8

--- a/solution.py
+++ b/solution.py
@@ -20,7 +20,7 @@
 XPARTS = 2
 BUFS = 4
 SLOTS = 4
-RING1, RING = 16, 8
+RING1, RING = 12, 6
 PARTS = 4
 
 

time: 210 us -> 210 us (level)
  no operation moved by 1% of the time
where the time goes in v9:
time: 210 us
  Pallas kernels  210 us (100%)
    pallas_call x1, Pallas kernels, exchange(): pl.pallas_call(functools.partial(exchange_kernel, R, C), name='exchange',...  203 us
    pallas_call x1, Pallas kernels, last(): pl.pallas_call(last_kernel, name='last', out_shape=jax.ShapeDtypeStruct((...  6.83 us

profile of v9, /device:TPU:97, one launch (start us, length us, event | category | flops | bytes accessed | tf_op | source)
XLA Modules:
  0.0 209.9 jit_solution(7520046774931207660)
XLA Ops:
  0.0 202.9 %exchange.1 = (bf16[64,448,128]{2,1,0:T(8,128)(2,1)S(1)}, bf16[64,64,128]{2,1,0:T(8,128)(2,1)S(1)}, bf16[512,512]{1,0:T(8,128)(2,1)S(1)}) custom-call(bf16[512,64,128]{2,1,0:T(8,128)(2,1)} %bitcast.2, bf16[512,512]{1,0:T(8,128)(2,1)} %a_hbm.1, bf16[512,512]{1,0:T(8,128)(2,1)} %b_hbm.1, bf16[512,512]{1,0:T(8,128)(2,1)} %c_hbm.1, f32[64,128,512]{2,1,0:T(8,128)} %d.1), custom_call_target="tpu_custom_call" | custom-call | tf_op jit(solution)/shard_map/exchange/pallas_call | solution.py:324
  202.9 6.8 %last.1 = f32[512,64,128]{2,1,0:T(8,128)} custom-call(bf16[512,512]{1,0:T(8,128)(2,1)S(1)} %get-tuple-element.8.at, bf16[64,448,128]{2,1,0:T(8,128)(2,1)S(1)} %get-tuple-element.9.h, bf16[64,64,128]{2,1,0:T(8,128)(2,1)S(1)} %get-tuple-element.10.hb), custom_call_target="tpu_custom_call" | custom-call | tf_op jit(solution)/shard_map/last/pallas_call | solution.py:388
